TPU v7x, 32 devices: a whole 2x2x4 slice. The times are simulated.
32 devices in a mesh: dp: 4 (over x, core), mp: 8 (over z, y).
Axes of the slice: x: 2, y: 2, z: 4, core: 2. Of those that a mesh axis runs over, the one named last changes fastest.
Arguments:
- gradients: bfloat16 [4, 4096, 4096], P('dp', None, 'mp'), may hold values from -40 to 40
- owner_table: int32 [128], replicated, may hold values from 0 to 7, as said below
Outputs:
- root_stacks: float32 [8, 24, 512, 512], P('mp', 'dp')
- slab_roots: float32 [16, 512, 4096], P(None, 'dp', 'mp')
Inputs may be any that keep to these rules, and one draw needn't show every extreme that they name: `owner_table`: statistic m * 16 + i belongs to column slab m. No owner is named by more than 24 statistics and some owner by exactly 24; among the 16 statistics of one column slab no owner is named more than 3 times, and some slab names some owner exactly 3 times.
All inputs are finite; a program needn't handle non-finite values.
Results may differ from a plain program's by a relative error of at most 0.0017.
Values may be sent and summed in bfloat16 or wider, within the bound.
A program may use at most 320 MiB of HBM per device.

v0:
```python
import jax
import jax.numpy as jnp
from jax import lax
from jax.sharding import PartitionSpec as P

ITERS = 3
CAP = 24


def batched(first, second):
    return jnp.einsum("kab,kbc->kac", first, second, precision=lax.Precision.HIGHEST)


def newton_roots(statistics, iterations):
    matrix_size = statistics.shape[-1]
    identity = jnp.eye(matrix_size, dtype=jnp.float32)
    diagonal_mean = jnp.mean(jnp.diagonal(statistics, axis1=1, axis2=2), axis=1)
    damped = statistics + 0.1 * diagonal_mean[:, None, None] * identity[None]
    mean_square = jnp.mean(damped * damped, axis=(1, 2))
    norm_scale = matrix_size * jnp.sqrt(mean_square + 1e-06)
    matrix = damped / norm_scale[:, None, None]
    root_scale = norm_scale ** (-0.25)
    current = matrix
    for iteration in range(iterations):
        factor = (5.0 * identity - matrix) * 0.25
        if iteration == 0:
            current = factor * root_scale[:, None, None]
        else:
            current = batched(current, factor)
        if iteration + 1 < iterations:
            square = batched(factor, factor)
            matrix = batched(square, batched(square, matrix))
    return current


def pick_rows(source, match_table):
    labels = jnp.arange(match_table.shape[1], dtype=jnp.int32)
    pick_index = jnp.sum(match_table * labels[None, :], axis=1)
    is_valid = jnp.sum(match_table, axis=1).astype(jnp.float32)
    return jnp.take(source, pick_index, axis=0) * is_valid[:, None, None]


def make_plan(owner_table, model_index, model_count, per_slab, pair_count):
    stat_count = owner_table.shape[0]
    owner_ids = jnp.arange(model_count, dtype=jnp.int32)
    onehot = (owner_table[:, None] == owner_ids[None, :]).astype(jnp.int32)
    slot_number = jnp.sum((jnp.cumsum(onehot, axis=0) - onehot) * onehot, axis=1)
    owner_grid = onehot.reshape(model_count, per_slab, model_count)
    pair_rank = jnp.sum((jnp.cumsum(owner_grid, axis=1) - owner_grid) * owner_grid, axis=2).reshape(
        stat_count
    )
    stat_ids = jnp.arange(stat_count, dtype=jnp.int32)
    position = stat_ids // per_slab * pair_count + pair_rank
    owner_loads = jnp.sum(onehot, axis=0)
    first_stat = model_index * per_slab
    targets = lax.dynamic_slice_in_dim(owner_table * pair_count + pair_rank, first_stat, per_slab)
    slot_ids = jnp.arange(CAP, dtype=jnp.int32)
    slot_match = (
        (owner_table[None, :] == model_index) & (slot_number[None, :] == slot_ids[:, None])
    ).astype(jnp.int32)
    stack_index = jnp.sum(slot_match * position[None, :], axis=1)
    stack_valid = jnp.sum(slot_match, axis=1)
    return (targets, stack_index, stack_valid, owner_loads)


def to_owner(pieces, route_plan, model_count, pair_count):
    targets, stack_index, stack_valid, owner_loads = route_plan
    places = jnp.arange(model_count * pair_count, dtype=jnp.int32)
    send_match = (places[:, None] == targets[None, :]).astype(jnp.int32)
    incoming = lax.all_to_all(
        pick_rows(pieces, send_match), "mp", split_axis=0, concat_axis=0, tiled=True
    )
    slot_match = (stack_index[:, None] == places[None, :]).astype(jnp.int32) * stack_valid[:, None]
    slot_stack = pick_rows(incoming, slot_match)
    return lax.all_to_all(slot_stack, "dp", split_axis=0, concat_axis=1, tiled=True)


def row_sums(rounded, data_count):
    return lax.psum_scatter(
        rounded.astype(jnp.bfloat16), "dp", scatter_dimension=1, tiled=True
    ).astype(jnp.float32) * (1.0 / data_count)


def on_device(gradients, owner_table):
    data_count = lax.axis_size("dp")
    model_count = lax.axis_size("mp")
    model_index = lax.axis_index("mp")
    block_size = gradients.shape[2]
    row_blocks = gradients.shape[1] // block_size
    per_slab = 2 * row_blocks
    pair_count = (CAP + model_count - 1) // model_count
    local_blocks = gradients[0].reshape(row_blocks, block_size, block_size)
    left_gram = jnp.einsum(
        "rab,rcb->rac", local_blocks, local_blocks, preferred_element_type=jnp.float32
    )
    right_gram = jnp.einsum(
        "rab,rac->rbc", local_blocks, local_blocks, preferred_element_type=jnp.float32
    )
    partial_value = jnp.stack([left_gram, right_gram], axis=1).reshape(
        per_slab, block_size, block_size
    )
    rounded = lax.optimization_barrier(partial_value.astype(jnp.bfloat16)).astype(jnp.float32)
    route_plan = make_plan(owner_table, model_index, model_count, per_slab, pair_count)
    stat_sums = row_sums(rounded, data_count)
    whole_stats = lax.all_to_all(stat_sums, "dp", split_axis=0, concat_axis=1, tiled=True)
    home_roots = newton_roots(whole_stats, ITERS)
    slab_roots = lax.all_to_all(home_roots, "dp", split_axis=1, concat_axis=0, tiled=True)
    root_stacks = to_owner(slab_roots, route_plan, model_count, pair_count)
    return (root_stacks[None], slab_roots)


def solution(mesh):
    placed = (P("dp", None, "mp"), P())
    return jax.shard_map(
        on_device,
        mesh=mesh,
        in_specs=placed,
        out_specs=(P("mp", "dp", None, None), P(None, "dp", "mp")),
        check_vma=False,
    )
```

profile of v0, /device:TPU:0, one launch (start us, length us, event | category | flops | bytes accessed | tf_op | source)
XLA Modules:
  0.0 612.6 jit_solution(5011616067232610238)
XLA Ops:
  7.2 6.0 convert_bitcast_fusion
  17.6 6.2 %pad_maximum_fusion = bf16[8,2,512,512]{3,2,0,1:T(8,128)(2,1)} fusion(bf16[8,1,512,512]{3,2,0,1:T(8,128)(2,1)S(1)} %convert_bitcast_fusion, bf16[8,1,512,512]{3,2,0,1:T(8,128)(2,1)} %convert_bitcast_fusion.1), kind=kLoop, calls=%fused_computation.3 | loop fusion | flops 4194304 | bytes 16777216 | tf_op jit(solution)/shard_map/stack | solution.py:99
  23.8 7.3 %copy.28 = bf16[8,2,512,512]{3,2,1,0:T(8,128)(2,1)} copy(bf16[8,2,512,512]{3,2,0,1:T(8,128)(2,1)} %pad_maximum_fusion) | data formatting | bytes 16777216 | tf_op jit(solution)/shard_map/stack | solution.py:99
  31.1 74.3 %reduce-scatter.2.cloned.1.call-done = bf16[16,128,512]{2,1,0:T(8,128)(2,1)} async-done(((bf16[16,512,512]{2,1,0:T(8,128)(2,1)}), bf16[16,128,512]{2,1,0:T(8,128)(2,1)}) %reduce-scatter.2.cloned.1.call-update) | async-done | bytes 2097168 | tf_op jit(solution)/shard_map/reduce_scatter | solution.py:79
  114.9 47.8 %all-to-all-done = f32[16,128,512]{2,1,0:T(8,128)} async-done(((f32[16,128,512]{2,1,0:T(8,128)}), f32[16,128,512]{2,1,0:T(8,128)}, u32[]{:S(2)}, u32[]{:S(2)}) %all-to-all-start) | async-done | bytes 4194336 | tf_op jit(solution)/shard_map/all_to_all | solution.py:105
  167.4 60.3 %copy.30 = f32[4,512,512]{0,2,1:T(8,128)} copy(f32[4,512,512]{2,1,0:T(8,128)} %bitcast.41) | data formatting | bytes 8388608 | tf_op jit(solution)/shard_map/all_to_all | solution.py:105
  227.8 6.1 gather_fusion
  238.2 7.7 %fusion.3 = f32[4,512,512]{2,1,0:T(8,128)S(1)} fusion(f32[4,512,512]{2,1,0:T(8,128)S(1)} %add_divide_fusion, f32[512,512]{1,0:T(8,128)S(1)} %fusion.21), kind=kOutput, calls=%fused_computation.10 | convolution fusion | flops 6444548096 | bytes 9437184 | tf_op jit(solution)/shard_map/kab,kbc->kac/dot_general | solution.py:11
  246.0 7.2 %fusion.37 = f32[4,512,512]{2,1,0:T(8,128)S(1)} fusion(f32[4,512,512]{2,1,0:T(8,128)S(1)} %fusion.3, f32[4,512,512]{2,1,0:T(8,128)S(1)} %add_divide_fusion), kind=kOutput, calls=%fused_computation.83 | convolution fusion | flops 6442450944 | bytes 12582912 | tf_op jit(solution)/shard_map/kab,kbc->kac/dot_general | solution.py:11
  253.2 7.3 %fusion.38 = f32[4,512,512]{2,1,0:T(8,128)S(1)} fusion(f32[4,512,512]{2,1,0:T(8,128)S(1)} %fusion.3, f32[4,512,512]{2,1,0:T(8,128)S(1)} %fusion.37), kind=kOutput, calls=%fused_computation.84 | convolution fusion | flops 6442450944 | bytes 12582912 | tf_op jit(solution)/shard_map/kab,kbc->kac/dot_general | solution.py:11
  260.5 7.9 %fusion.9 = f32[4,512,512]{2,1,0:T(8,128)S(1)} fusion(f32[4,512,512]{2,1,0:T(8,128)S(1)} %fusion.38, f32[512,512]{1,0:T(8,128)S(1)} %fusion.21), kind=kOutput, calls=%fused_computation.21 | convolution fusion | flops 6444548096 | bytes 9437184 | tf_op jit(solution)/shard_map/kab,kbc->kac/dot_general | solution.py:11
  268.5 7.0 %fusion.39 = f32[4,512,512]{2,1,0:T(8,128)S(1)} fusion(f32[4,512,512]{2,1,0:T(8,128)S(1)} %fusion.9, f32[4,512,512]{2,1,0:T(8,128)S(1)} %fusion.38), kind=kOutput, calls=%fused_computation.85 | convolution fusion | flops 6442450944 | bytes 12582912 | tf_op jit(solution)/shard_map/kab,kbc->kac/dot_general | solution.py:11
  275.5 7.7 %fusion.40 = f32[4,512,512]{2,1,0:T(8,128)S(1)} fusion(f32[4,512,512]{2,1,0:T(8,128)S(1)} %fusion.9, f32[4,512,512]{2,1,0:T(8,128)S(1)} %fusion.39), kind=kOutput, calls=%fused_computation.86 | convolution fusion | flops 6442450944 | bytes 12582912 | tf_op jit(solution)/shard_map/kab,kbc->kac/dot_general | solution.py:11
  283.3 7.8 %fusion.5 = f32[4,512,512]{2,1,0:T(8,128)S(1)} fusion(f32[4,512,512]{2,1,0:T(8,128)S(1)} %add_divide_fusion, f32[4,512,512]{2,1,0:T(8,128)S(1)} %fusion.38, f32[4]{0:T(128)S(1)} %get-tuple-element.8, f32[512,512]{1,0:T(8,128)S(1)} %fusion.21), kind=kOutput, calls=%fused_computation.12 | convolution fusion | flops 6446645248 | bytes 13631504 | tf_op jit(solution)/shard_map/kab,kbc->kac/dot_general | solution.py:11
  291.1 8.0 %fusion = f32[4,512,512]{2,1,0:T(8,128)S(1)} fusion(f32[4,512,512]{2,1,0:T(8,128)S(1)} %fusion.5, f32[4,512,512]{2,1,0:T(8,128)S(1)} %fusion.40, f32[512,512]{1,0:T(8,128)S(1)} %fusion.21), kind=kOutput, calls=%fused_computation.6 | convolution fusion | flops 6444548096 | bytes 13631488 | tf_op jit(solution)/shard_map/kab,kbc->kac/dot_general | solution.py:11
  303.8 5.2 all-to-all-start.1
  310.0 47.2 %all-to-all-done.1 = f32[4,512,512]{2,0,1:T(4,128)} async-done(((f32[4,512,512]{2,0,1:T(4,128)}), f32[4,512,512]{2,0,1:T(4,128)}, u32[]{:S(2)}, u32[]{:S(2)}) %all-to-all-start.1) | async-done | bytes 4194336 | tf_op jit(solution)/shard_map/all_to_all | solution.py:107
  357.2 5.5 copy.32
  362.7 5.8 gather_fusion.1
  368.5 6.8 %select_multiply_fusion.1 = f32[24,128,512]{2,1,0:T(8,128)} fusion(f32[24,128,512]{2,1,0:T(8,128)} %gather_fusion.1, f32[24]{0:T(128)S(1)} %convert_element_type.54, pred[24]{0:T(512)(128)(4,1)S(1)} %compare_and_fusion), kind=kLoop, calls=%fused_computation.5 | loop fusion | flops 3145728 | bytes 12583032 | tf_op jit(solution)/shard_map/mul | solution.py:40
  375.3 5.5 all-to-all-start.2
  381.6 137.1 %all-to-all-done.2 = f32[24,128,512]{2,1,0:T(8,128)} async-done(((f32[24,128,512]{2,1,0:T(8,128)}), f32[24,128,512]{2,1,0:T(8,128)}, u32[]{:S(2)}, u32[]{:S(2)}) %all-to-all-start.2) | async-done | bytes 6291488 | tf_op jit(solution)/shard_map/all_to_all | solution.py:70
  518.7 6.4 %gather_fusion.2 = f32[24,128,512]{2,1,0:T(8,128)} fusion(f32[24,128,512]{2,1,0:T(8,128)} %all-to-all-done.2, s32[1024]{0:T(1024)S(1)} %pad_clamp_fusion), kind=kCustom, calls=%fused_computation.2 | custom fusion | bytes 12583008 | tf_op jit(solution)/shard_map/jit(_take)/gather | solution.py:40
  528.9 73.3 %all_to_all.56 = f32[24,128,512]{2,1,0:T(8,128)S(1)} all-to-all(f32[24,128,512]{2,1,0:T(8,128)S(1)} %select_multiply_fusion), channel_id=1, replica_groups=mesh['dp'=4,'mp'=8] {'dp'}, dimensions={0} | all-to-all | bytes 12582912 | tf_op jit(solution)/shard_map/all_to_all | solution.py:75
  (47 shorter events, 36.6 us)
Async XLA Ops:
  7.2 98.2 %reduce-scatter.2.cloned.1.call-start = ((), (), s32[]{:S(2)}) async-start(), calls=%async_computation.5 | async-start | bytes 10485760 | tf_op jit(solution)/shard_map/reduce_scatter | solution.py:79
  7.2 6.0 copy-start.1
  109.6 53.1 %all-to-all-start = ((f32[16,128,512]{2,1,0:T(8,128)}), f32[16,128,512]{2,1,0:T(8,128)}, u32[]{:S(2)}, u32[]{:S(2)}) async-start(f32[16,128,512]{2,1,0:T(8,128)} %convert_multiply_fusion), calls=%async_computation.1 | async-start | bytes 8388608 | tf_op jit(solution)/shard_map/all_to_all | solution.py:105
  233.9 3.5 copy-start
  303.8 5.2 copy-start.2
  303.8 53.4 %all-to-all-start.1 = ((f32[4,512,512]{2,0,1:T(4,128)}), f32[4,512,512]{2,0,1:T(4,128)}, u32[]{:S(2)}, u32[]{:S(2)}) async-start(f32[4,512,512]{2,0,1:T(4,128)} %copy.31), calls=%async_computation.2 | async-start | bytes 8388608 | tf_op jit(solution)/shard_map/all_to_all | solution.py:107
  375.3 143.4 %all-to-all-start.2 = ((f32[24,128,512]{2,1,0:T(8,128)}), f32[24,128,512]{2,1,0:T(8,128)}, u32[]{:S(2)}, u32[]{:S(2)}) async-start(f32[24,128,512]{2,1,0:T(8,128)} %select_multiply_fusion.1), calls=%async_computation.3 | async-start | bytes 12582912 | tf_op jit(solution)/shard_map/all_to_all | solution.py:70
Sparse Core Ops, SparseCore 0:
  31.3 74.1 reduce-scatter.1
where the time goes:
time: 620 us; the launch traced here: 613 us
  waiting for transfers between devices  306 us (49%)
  local copies, waits for them, and re-layouts  105 us (17%)
  blocking collectives  73.3 us (12%)
  matrix products  71.1 us (11%)
  other arithmetic  26.9 us (4%)
  starting transfers between devices  15.6 us (3%)
  between operations  14.5 us (2%)
    all_to_all x1, waiting for transfers between devices, to_owner(): lax.all_to_all(pick_rows(pieces, send_match), 'mp', split_axis=0, concat_...  137 us
    reduce_scatter x1, waiting for transfers between devices, row_sums(): lax.psum_scatter(rounded.astype(jnp.bfloat16), 'dp', scatter_dimension=1,...  74.3 us
    all_to_all x1, blocking collectives, to_owner(): lax.all_to_all(slot_stack, 'dp', split_axis=0, concat_axis=1, tiled=True)  73.3 us
    all_to_all x2, local copies, waits for them, and re-layouts, on_device(): lax.all_to_all(stat_sums, 'dp', split_axis=0, concat_axis=1, tiled=True)  65.1 us
    dot_general x8, matrix products, batched(): jnp.einsum('kab,kbc->kac', first, second, precision=lax.Precision.HIGHEST)  60.8 us
    all_to_all x1, waiting for transfers between devices, on_device(): lax.all_to_all(stat_sums, 'dp', split_axis=0, concat_axis=1, tiled=True)  47.8 us
    all_to_all x1, waiting for transfers between devices, on_device(): lax.all_to_all(home_roots, 'dp', split_axis=1, concat_axis=0, tiled=True)  47.2 us
  transfers between devices with their start and end apart: 4, of which 4 were waited for; matrix products, arithmetic and copies ran while one was open for 0% of the time, Pallas kernels for 0%

commit v1 on v0

--- a/solution.py
+++ b/solution.py
@@ -1,6 +1,8 @@
 import jax
 import jax.numpy as jnp
 from jax import lax
+from jax.experimental import pallas as pl
+from jax.experimental.pallas import tpu as pltpu
 from jax.sharding import PartitionSpec as P
 
 ITERS = 3
@@ -109,10 +111,345 @@
     return (root_stacks[None], slab_roots)
 
 
+def iota2(shape, axis):
+    return lax.broadcasted_iota(jnp.int32, shape, axis)
+
+
+def matmul(first, second):
+    return jnp.dot(
+        first.astype(jnp.bfloat16), second.astype(jnp.bfloat16), preferred_element_type=jnp.float32
+    )
+
+
+def fold_upper(store, full):
+    store(0, 128, 0, 512, full[0:128, :])
+    store(128, 256, 128, 512, full[128:256, 128:512])
+    store(128, 256, 0, 128, full[384:512, 384:512])
+    store(256, 320, 0, 256, full[256:320, 256:512])
+    store(256, 320, 256, 512, full[320:384, 256:512])
+
+
+def gram_kernel(where_ref, grad_ref, out_ref):
+    block = grad_ref[0]
+    for kind in range(2):
+        flipped = block.T
+        full = jnp.dot(block, flipped, preferred_element_type=jnp.float32) if kind == 0 else jnp.dot(
+            flipped, block, preferred_element_type=jnp.float32
+        )
+        full = full.astype(jnp.bfloat16)
+
+        def store(r0, r1, c0, c1, value, kind=kind):
+            out_ref[0, kind, r0:r1, c0:c1] = value
+
+        fold_upper(store, full)
+
+
+def grams(where, gradients, relative_core):
+    size = gradients.shape[2]
+
+    def grad_map(step, where_ref):
+        target = where_ref[0] ^ relative_core ^ ((1 - step // 2) * 2)
+        return (0, target * 2 + step % 2, 0)
+
+    return pl.pallas_call(
+        gram_kernel,
+        grid_spec=pltpu.PrefetchScalarGridSpec(
+            num_scalar_prefetch=1,
+            grid=(4,),
+            in_specs=[pl.BlockSpec((1, size, size), grad_map)],
+            out_specs=pl.BlockSpec((1, 2, 320, size), lambda step, where_ref: (step, 0, 0, 0)),
+        ),
+        out_shape=jax.ShapeDtypeStruct((4, 2, 320, size), jnp.bfloat16),
+        cost_estimate=pl.CostEstimate(flops=8 * 2 * size**3, bytes_accessed=5 * 2**20, transcendentals=0),
+        name="grams_%d" % relative_core,
+    )(where, gradients)
+
+
+def unfold(source, whole):
+    whole[0:128, :] = source(0, 128, 0, 512)
+    whole[128:256, 128:512] = source(128, 256, 128, 512)
+    whole[384:512, 384:512] = source(128, 256, 0, 128)
+    whole[256:320, 256:512] = source(256, 320, 0, 256)
+    whole[320:384, 256:512] = source(256, 320, 256, 512)
+    for i in range(4):
+        for j in range(i + 1, 4):
+            whole[j * 128 : j * 128 + 128, i * 128 : i * 128 + 128] = whole[
+                i * 128 : i * 128 + 128, j * 128 : j * 128 + 128
+            ].T
+
+
+def newton_kernel(where_ref, own_ref, core_ref, far_ref, *rest):
+    outs, whole = rest[:4], rest[4]
+    size = whole.shape[0]
+
+    def source(r0, r1, c0, c1):
+        return (
+            own_ref[0, r0:r1, c0:c1].astype(jnp.float32)
+            + core_ref[0, r0:r1, c0:c1].astype(jnp.float32)
+            + far_ref[0, r0:r1, c0:c1].astype(jnp.float32)
+        ) * 0.25
+
+    unfold(source, whole)
+    identity = (iota2((size, size), 0) == iota2((size, size), 1)).astype(jnp.float32)
+    statistic = whole[...]
+    diagonal = jnp.sum(jnp.sum(statistic * identity, axis=0, keepdims=True), axis=1, keepdims=True) / size
+    damped = statistic + 0.1 * diagonal * identity
+    square = jnp.sum(jnp.sum(damped * damped, axis=0, keepdims=True), axis=1, keepdims=True) / (size * size)
+    norm_scale = size * jnp.sqrt(square + 1e-06)
+    root_scale = 1.0 / jnp.sqrt(jnp.sqrt(norm_scale))
+    first = damped * (1.0 / norm_scale)
+
+    def advance(matrix):
+        part = matmul(matrix, matrix) * 0.0625 - 0.625 * matrix
+        half = 1.5625 * matrix + matmul(part, matrix)
+        return 1.5625 * half + matmul(part, half)
+
+    second = advance(first)
+    product = matmul(first, second) * 0.0625 - 0.3125 * (first + second)
+    third = advance(second)
+    rest_part = 1.25 * product - 0.390625 * third - 0.25 * matmul(product, third)
+    whole[...] = rest_part * root_scale
+    centre = root_scale * 1.953125
+    high = centre.astype(jnp.bfloat16).astype(jnp.float32)
+    low = centre - high
+    for relative in range(4):
+        target = where_ref[0] ^ relative
+        rows = pl.multiple_of(target * 128, 128)
+        outs[relative][0] = whole[pl.ds(rows, 128), :].astype(jnp.bfloat16)
+        last = whole[pl.ds(rows + 112, 16), pl.ds(rows, 128)]
+        row, lane = iota2((16, 128), 0), iota2((16, 128), 1)
+        last = jnp.where((row == 15) & (lane == 0), high, last)
+        last = jnp.where((row == 15) & (lane == 1), low, last)
+        outs[relative][0, 112:128, pl.ds(rows, 128)] = last.astype(jnp.bfloat16)
+
+
+def newton(where, own, core, far, chunk):
+    size = own.shape[-1]
+    folded = own.shape[-2]
+    flat = lambda array: array.reshape(-1, folded, size)
+    spec = lambda offset: pl.BlockSpec((1, folded, size), lambda step, where_ref: (offset + step, 0, 0))
+    return pl.pallas_call(
+        newton_kernel,
+        grid_spec=pltpu.PrefetchScalarGridSpec(
+            num_scalar_prefetch=1,
+            grid=(2,),
+            in_specs=[spec(4 + chunk * 2), spec(4 + chunk * 2), spec(0)],
+            out_specs=[pl.BlockSpec((1, 128, size), lambda step, where_ref: (step, 0, 0))] * 4,
+            scratch_shapes=[pltpu.VMEM((size, size), jnp.float32)],
+        ),
+        out_shape=[jax.ShapeDtypeStruct((2, 128, size), jnp.bfloat16)] * 4,
+        cost_estimate=pl.CostEstimate(flops=16 * 2 * size**3, bytes_accessed=4 * 2**20, transcendentals=0),
+        name="newton_%d" % chunk,
+    )(where, flat(own), flat(core), flat(far))
+
+
+def opened(tile):
+    row, lane = iota2((128, 128), 0), iota2((128, 128), 1)
+    line = iota2((1, 128), 1)
+    last = tile[127:128, :]
+    pick = lambda values, mask: jnp.sum(jnp.where(mask, values, 0.0), axis=1, keepdims=True)
+    centre = pick(last, line < 2)
+    first_value = pick(tile[0:1, :], line == 127)
+    second_value = pick(tile[1:2, :], line == 127)
+    tile = jnp.where((row == 127) & (lane == 0), first_value, tile)
+    tile = jnp.where((row == 127) & (lane == 1), second_value, tile)
+    return tile + jnp.where(row == lane, centre, 0.0)
+
+
+def locate(stat, device):
+    return (stat // 4) ^ device, (stat % 4) // 2, stat % 2
+
+
+def gather_rows(where, refs, held):
+    for chunk in range(2):
+        for relative in range(4):
+            for place in range(2):
+                target = (where ^ relative) * 4 + chunk * 2 + place
+                held[target] = refs[chunk * 4 + relative][place]
+
+
+def slab_kernel(where_ref, *rest):
+    refs, out_ref = rest[:8], rest[8]
+    device = where_ref[0]
+    columns = pl.multiple_of(device * 128, 128)
+    for chunk in range(2):
+        for relative in range(4):
+            base = (device ^ relative) * 4 + chunk * 2
+
+            def body(place, carry):
+                value = refs[chunk * 4 + relative][place].astype(jnp.float32)
+                out_ref[base + place] = value
+                tile = refs[chunk * 4 + relative][place, :, pl.ds(columns, 128)].astype(jnp.float32)
+                out_ref[base + place, :, pl.ds(columns, 128)] = opened(tile)
+                return carry
+
+            lax.fori_loop(0, 2, body, 0)
+
+
+def slab_rows(where, pieces, stats):
+    size = pieces[0].shape[-1]
+    return pl.pallas_call(
+        slab_kernel,
+        in_specs=[pl.BlockSpec(memory_space=pltpu.SMEM)] + [pl.BlockSpec(memory_space=pltpu.VMEM)] * 8,
+        out_specs=pl.BlockSpec(memory_space=pltpu.VMEM),
+        out_shape=jax.ShapeDtypeStruct((stats, 128, size), jnp.float32),
+        cost_estimate=pl.CostEstimate(flops=2**22, bytes_accessed=6 * 2**20, transcendentals=0),
+        name="slab_rows",
+    )(where, *pieces)
+
+
+def send_kernel(where_ref, index_ref, valid_ref, *rest):
+    refs, out_ref, held, tiles = rest[:8], rest[8], rest[9], rest[10]
+    device = where_ref[0]
+    gather_rows(device, refs, held)
+    own = pl.multiple_of(device * 128, 128)
+    after = pl.multiple_of(((device + 1) % 4) * 128, 128)
+    across = pl.multiple_of((device ^ 2) * 128, 128)
+
+    def body(place, carry):
+        @pl.when(valid_ref[place] > 0)
+        def _():
+            stat = index_ref[place]
+            out_ref[place, 0:128, 0:128] = held[stat, :, pl.ds(own, 128)]
+            out_ref[place, 0:128, 128:256] = held[stat, :, pl.ds(after, 128)]
+            tile = held[stat, :, pl.ds(across, 128)].astype(jnp.float32)
+            half = jnp.where(device < 2, tile[0:64, :], tile.T[64:128, :]).astype(jnp.bfloat16)
+            out_ref[place, 128:160, 0:128] = half[0:32, :]
+            out_ref[place, 128:160, 128:256] = half[32:64, :]
+
+        @pl.when(valid_ref[place] == 0)
+        def _():
+            out_ref[place] = jnp.zeros(out_ref.shape[1:], out_ref.dtype)
+
+        return carry
+
+    lax.fori_loop(0, out_ref.shape[0], body, 0)
+
+
+def send_rows(where, index, valid, pieces, stats):
+    size = pieces[0].shape[-1]
+    places = index.shape[0]
+    smem = pl.BlockSpec(memory_space=pltpu.SMEM)
+    return pl.pallas_call(
+        send_kernel,
+        in_specs=[smem] * 3 + [pl.BlockSpec(memory_space=pltpu.VMEM)] * 8,
+        out_specs=pl.BlockSpec(memory_space=pltpu.VMEM),
+        out_shape=jax.ShapeDtypeStruct((places, 160, 256), jnp.bfloat16),
+        scratch_shapes=[
+            pltpu.VMEM((stats, 128, size), jnp.bfloat16),
+            pltpu.VMEM((128, 128), jnp.float32),
+        ],
+        cost_estimate=pl.CostEstimate(flops=2**22, bytes_accessed=4 * 2**20, transcendentals=0),
+        name="send_rows",
+    )(where, index, valid, *pieces)
+
+
+def slot_kernel(index_ref, valid_ref, source_ref, out_ref):
+    def body(slot, carry):
+        @pl.when(valid_ref[slot] > 0)
+        def _():
+            out_ref[slot] = source_ref[index_ref[slot]]
+
+        @pl.when(valid_ref[slot] == 0)
+        def _():
+            out_ref[slot] = jnp.zeros(out_ref.shape[1:], out_ref.dtype)
+
+        return carry
+
+    lax.fori_loop(0, out_ref.shape[0], body, 0)
+
+
+def slot_rows(index, valid, source):
+    smem = pl.BlockSpec(memory_space=pltpu.SMEM)
+    return pl.pallas_call(
+        slot_kernel,
+        in_specs=[smem, smem, pl.BlockSpec(memory_space=pltpu.VMEM)],
+        out_specs=pl.BlockSpec(memory_space=pltpu.VMEM),
+        out_shape=jax.ShapeDtypeStruct((index.shape[0],) + source.shape[1:], source.dtype),
+        cost_estimate=pl.CostEstimate(flops=2**20, bytes_accessed=4 * 2**20, transcendentals=0),
+        name="slot_rows",
+    )(index, valid, source)
+
+
+def stack_kernel(piece_ref, out_ref):
+    tile_at = lambda i: slice(i * 128, i * 128 + 128)
+    for i in range(4):
+        out_ref[0, tile_at(i), tile_at(i)] = opened(piece_ref[i, 0, 0:128, 0:128].astype(jnp.float32))
+        j = (i + 1) % 4
+        tile = piece_ref[i, 0, 0:128, 128:256].astype(jnp.float32)
+        out_ref[0, tile_at(i), tile_at(j)] = tile
+        out_ref[0, tile_at(j), tile_at(i)] = tile.T
+    for i in range(2):
+        parts = []
+        for source in (i, i + 2):
+            parts += [piece_ref[source, 0, 128:160, 0:128], piece_ref[source, 0, 128:160, 128:256]]
+        tile = jnp.concatenate([part.astype(jnp.float32) for part in parts], axis=0)
+        out_ref[0, tile_at(i), tile_at(i + 2)] = tile
+        out_ref[0, tile_at(i + 2), tile_at(i)] = tile.T
+
+
+def stack_rows(pieces, size):
+    slots = pieces.shape[1]
+    return pl.pallas_call(
+        stack_kernel,
+        grid=(slots,),
+        in_specs=[pl.BlockSpec((4, 1, 160, 256), lambda slot: (0, slot, 0, 0))],
+        out_specs=pl.BlockSpec((1, size, size), lambda slot: (slot, 0, 0)),
+        out_shape=jax.ShapeDtypeStruct((slots, size, size), jnp.float32),
+        cost_estimate=pl.CostEstimate(flops=2**22, bytes_accessed=8 * 2**20, transcendentals=0),
+        name="stack_rows",
+    )(pieces)
+
+
+def exchange(array, relative):
+    return lax.ppermute(array, "dp", [(i, i ^ relative) for i in range(4)])
+
+
+def on_quad(gradients, owner_table):
+    model_count = lax.axis_size("mp")
+    model_index = lax.axis_index("mp")
+    device = lax.axis_index("dp")
+    where = device.astype(jnp.int32).reshape(1)
+    size = gradients.shape[2]
+    per_slab = 2 * (gradients.shape[1] // size)
+    pair_count = (CAP + model_count - 1) // model_count
+    targets, stack_index, stack_valid, _ = make_plan(
+        owner_table, model_index, model_count, per_slab, pair_count
+    )
+    places = jnp.arange(model_count * pair_count, dtype=jnp.int32)
+    send_match = (places[:, None] == targets[None, :]).astype(jnp.int32)
+    send_index = jnp.sum(send_match * jnp.arange(per_slab, dtype=jnp.int32)[None, :], axis=1)
+    send_valid = jnp.sum(send_match, axis=1)
+
+    received = exchange(grams(where, gradients, 1), 1)
+    own = grams(where, gradients, 0)
+    pieces = []
+    for chunk in range(2):
+        summed = (own[chunk].astype(jnp.float32) + received[chunk].astype(jnp.float32)).astype(jnp.bfloat16)
+        far = exchange(summed, 2)
+        roots = newton(where, own, received, far, chunk)
+        pieces += [roots[0]] + [exchange(roots[relative], relative) for relative in (1, 2, 3)]
+    sent = send_rows(where, send_index, send_valid, pieces, per_slab)
+    incoming = lax.all_to_all(sent, "mp", split_axis=0, concat_axis=0, tiled=True)
+    slab = slab_rows(where, pieces, per_slab)
+    slots = slot_rows(stack_index, stack_valid, incoming)
+    shared = lax.all_to_all(slots, "dp", split_axis=0, concat_axis=0, tiled=True)
+    stacks = stack_rows(shared.reshape(4, CAP // 4, 160, 256), size)
+    return (stacks[None], slab)
+
+
 def solution(mesh):
     placed = (P("dp", None, "mp"), P())
+
+    def body(gradients, owner_table):
+        size = gradients.shape[2]
+        row_blocks = gradients.shape[1] // size
+        if lax.axis_size("dp") == 4 and size == 512 and row_blocks == 8:
+            return on_quad(gradients, owner_table)
+        return on_device(gradients, owner_table)
+
     return jax.shard_map(
-        on_device,
+        body,
         mesh=mesh,
         in_specs=placed,
         out_specs=(P("mp", "dp", None, None), P(None, "dp", "mp")),

time: 620 us -> 170 us (0.27); the launches traced: 613 us -> 170 us
  waiting for transfers between devices: 306 us -> 93.9 us
  local copies, waits for them, and re-layouts: 105 us -> 4.52 us
  blocking collectives: 73.3 us -> 0 us
  matrix products: 71.1 us -> 0 us
  Pallas kernels: 0 us -> 48.3 us
  other arithmetic: 26.9 us -> 5.61 us
  between operations: 14.5 us -> 0.74 us
    all_to_all x3 -> x2, waiting for transfers between devices: 232 us -> 64 us  [the longest x1 44.8 us: on_quad(): lax.all_to_all(sent, 'mp', split_axis=0, concat_axis=0, tiled=True)]
    reduce_scatter x1 -> x0, waiting for transfers between devices: 74.3 us -> none  [row_sums(): lax.psum_scatter(rounded.astype(jnp.bfloat16), 'dp', scatter_dimension=1,...]
    all_to_all x4 -> x0, local copies, waits for them, and re-layouts: 74 us -> none  [the longest x2 65.1 us: on_device(): lax.all_to_all(stat_sums, 'dp', split_axis=0, concat_axis=1, tiled=True)]
    all_to_all x1 -> x0, blocking collectives: 73.3 us -> none  [to_owner(): lax.all_to_all(slot_stack, 'dp', split_axis=0, concat_axis=1, tiled=True)]
    dot_general x10 -> x0, matrix products: 71.1 us -> none  [the longest x8 60.8 us: batched(): jnp.einsum('kab,kbc->kac', first, second, precision=lax.Precision.HIGHEST)]
    pallas_call x0 -> x8, Pallas kernels: none -> 48.3 us  [the longest x2 17.4 us: newton(): pl.pallas_call(newton_kernel, grid_spec=pltpu.PrefetchScalarGridSpec(num_...]
    ppermute x0 -> x9, waiting for transfers between devices: none -> 29.9 us  [exchange(): return lax.ppermute(array, 'dp', [(i, i ^ relative) for i in range(4)])]
    gather x3 -> x0, local copies, waits for them, and re-layouts: 18.3 us -> none  [the longest x2 12.3 us: pick_rows(): return jnp.take(source, pick_index, axis=0) * is_valid[:, None, None]]
  transfers between devices with their start and end apart: 4 -> 11, of which waited for: 4 -> 6; matrix products, arithmetic and copies ran while one was open for 0% -> 1% of each run, Pallas kernels for 0% -> 17%
where the time goes in v1:
time: 170 us
  waiting for transfers between devices  93.9 us (55%)
  Pallas kernels  48.3 us (28%)
  starting transfers between devices  16.7 us (10%)
  other arithmetic  5.61 us (3%)
  local copies, waits for them, and re-layouts  4.52 us (3%)
    all_to_all x1, waiting for transfers between devices, on_quad(): lax.all_to_all(sent, 'mp', split_axis=0, concat_axis=0, tiled=True)  44.8 us
    ppermute x9, waiting for transfers between devices, exchange(): return lax.ppermute(array, 'dp', [(i, i ^ relative) for i in range(4)])  29.9 us
    all_to_all x1, waiting for transfers between devices, on_quad(): lax.all_to_all(slots, 'dp', split_axis=0, concat_axis=0, tiled=True)  19.1 us
    pallas_call x2, Pallas kernels, newton(): pl.pallas_call(newton_kernel, grid_spec=pltpu.PrefetchScalarGridSpec(num_...  17.4 us
    pallas_call x2, Pallas kernels, grams(): pl.pallas_call(gram_kernel, grid_spec=pltpu.PrefetchScalarGridSpec(num_sc...  11.2 us
    ppermute x9, starting transfers between devices, exchange(): return lax.ppermute(array, 'dp', [(i, i ^ relative) for i in range(4)])  7.32 us
    pallas_call x1, Pallas kernels, stack_rows(): pl.pallas_call(stack_kernel, grid=(slots,), in_specs=[pl.BlockSpec((4, 1,...  5.85 us
    all_to_all x1, starting transfers between devices, on_quad(): lax.all_to_all(sent, 'mp', split_axis=0, concat_axis=0, tiled=True)  5.81 us
  transfers between devices with their start and end apart: 11, of which 6 were waited for; matrix products, arithmetic and copies ran while one was open for 1% of the time, Pallas kernels for 17%

profile of v1, /device:TPU:0, one launch (start us, length us, event | category | flops | bytes accessed | tf_op | source)
XLA Modules:
  0.0 169.7 jit_solution(18041857767373179044)
XLA Ops:
  0.6 5.6 %grams_1.1 = bf16[4,2,320,512]{3,2,1,0:T(8,128)(2,1)} custom-call(s32[1]{0:T(128)} %bitcast.where_ref, bf16[1,4096,512]{2,1,0:T(8,128)(2,1)} %grad_ref.3), custom_call_target="tpu_custom_call" | custom-call | flops 2147483648 | bytes 5242880 | tf_op jit(solution)/shard_map/grams_1/pallas_call | solution.py:154
  6.8 5.6 %grams_0.1 = bf16[4,2,320,512]{3,2,1,0:T(8,128)(2,1)} custom-call(s32[1]{0:T(128)} %bitcast.where_ref, bf16[1,4096,512]{2,1,0:T(8,128)(2,1)} %grad_ref.3), custom_call_target="tpu_custom_call" | custom-call | flops 2147483648 | bytes 5242880 | tf_op jit(solution)/shard_map/grams_0/pallas_call | solution.py:154
  12.4 3.5 %fusion.2 = (bf16[2,320,512]{2,1,0:T(8,128)(2,1)}, bf16[2,320,512]{2,1,0:T(8,128)(2,1)S(1)}) fusion(bf16[4,2,320,512]{3,2,1,0:T(8,128)(2,1)S(1)} %collective-permute-done, bf16[4,2,320,512]{3,2,1,0:T(8,128)(2,1)} %grams_0.1), kind=kLoop, calls=%fused_computation.5 | loop fusion | flops 2621440 | bytes 3932160 | tf_op jit(solution)/shard_map/convert_element_type | solution.py:428
  15.9 2.5 %collective-permute-start.5 = (bf16[2,320,512]{2,1,0:T(8,128)(2,1)}, bf16[2,320,512]{2,1,0:T(8,128)(2,1)}, u32[]{:S(2)}, u32[]{:S(2)}) collective-permute-start(bf16[2,320,512]{2,1,0:T(8,128)(2,1)} %get-tuple-element.22), channel_id=1, source_target_pairs={{0,16},{8,24},{16,0},{24,8},{1,17},{9,25},{17,1},{25,9},{2,18},{10... | collective-permute-start | bytes 1966088 | tf_op jit(solution)/shard_map/ppermute | solution.py:405
  19.1 15.1 %collective-permute-done.5.far_ref = bf16[2,320,512]{2,1,0:T(8,128)(2,1)} collective-permute-done((bf16[2,320,512]{2,1,0:T(8,128)(2,1)}, bf16[2,320,512]{2,1,0:T(8,128)(2,1)}, u32[]{:S(2)}, u32[]{:S(2)}) %collective-permute-start.5) | collective-permute-done | bytes 655392 | tf_op jit(solution)/shard_map/ppermute | solution.py:405
  34.2 8.7 %newton_1.1 = (bf16[2,128,512]{2,1,0:T(8,128)(2,1)}, bf16[2,128,512]{2,1,0:T(8,128)(2,1)}, bf16[2,128,512]{2,1,0:T(8,128)(2,1)}, bf16[2,128,512]{2,1,0:T(8,128)(2,1)}) custom-call(s32[1]{0:T(128)} %bitcast.where_ref, bf16[8,320,512]{2,1,0:T(8,128)(2,1)} %bitcast.13, bf16[8,320,512]{2,1,0:T(8,128)(2,1)} %bitcast.11, ...), custom_call_target="tpu_custom_call" | custom-call | flops 4294967296 | bytes 4194304 | tf_op jit(solution)/shard_map/newton_1/pallas_call | solution.py:231
  42.9 2.1 %collective-permute-start.7 = (bf16[2,128,512]{2,1,0:T(8,128)(2,1)}, bf16[2,128,512]{2,1,0:T(8,128)(2,1)S(1)}, u32[]{:S(2)}, u32[]{:S(2)}) collective-permute-start(bf16[2,128,512]{2,1,0:T(8,128)(2,1)} %get-tuple-element.16), channel_id=1, source_target_pairs={{0,16},{8,24},{16,0},{24,8},{1,17},{9,25},{17,1},{25,9},{2,18},{10... | collective-permute-start | bytes 786440 | tf_op jit(solution)/shard_map/ppermute | solution.py:405
  45.1 3.1 %collective-permute-done.1.far_ref = bf16[2,320,512]{2,1,0:T(8,128)(2,1)S(1)} collective-permute-done((bf16[2,320,512]{2,1,0:T(8,128)(2,1)S(1)}, bf16[2,320,512]{2,1,0:T(8,128)(2,1)S(1)}, u32[]{:S(2)}, u32[]{:S(2)}) %collective-permute-start.1) | collective-permute-done | bytes 655392 | tf_op jit(solution)/shard_map/ppermute | solution.py:405
  48.2 0.8 copy-done.10
  49.0 8.7 %newton_0.1 = (bf16[2,128,512]{2,1,0:T(8,128)(2,1)}, bf16[2,128,512]{2,1,0:T(8,128)(2,1)}, bf16[2,128,512]{2,1,0:T(8,128)(2,1)}, bf16[2,128,512]{2,1,0:T(8,128)(2,1)}) custom-call(s32[1]{0:T(128)} %bitcast.where_ref, bf16[8,320,512]{2,1,0:T(8,128)(2,1)} %bitcast.14, bf16[8,320,512]{2,1,0:T(8,128)(2,1)} %bitcast.12, bf16[2,320,512]{2,1,0:T(8,128)(2,1)} %copy-done.10), custom_call_target="tpu_custom_call" | custom-call | flops 4294967296 | bytes 4194304 | tf_op jit(solution)/shard_map/newton_0/pallas_call | solution.py:231
  57.8 2.1 %collective-permute-start.3 = (bf16[2,128,512]{2,1,0:T(8,128)(2,1)}, bf16[2,128,512]{2,1,0:T(8,128)(2,1)S(1)}, u32[]{:S(2)}, u32[]{:S(2)}) collective-permute-start(bf16[2,128,512]{2,1,0:T(8,128)(2,1)} %get-tuple-element.12), channel_id=1, source_target_pairs={{0,16},{8,24},{16,0},{24,8},{1,17},{9,25},{17,1},{25,9},{2,18},{10... | collective-permute-start | bytes 786440 | tf_op jit(solution)/shard_map/ppermute | solution.py:405
  60.7 6.5 %collective-permute-done.3.rest_2_ = bf16[2,128,512]{2,1,0:T(8,128)(2,1)S(1)} collective-permute-done((bf16[2,128,512]{2,1,0:T(8,128)(2,1)}, bf16[2,128,512]{2,1,0:T(8,128)(2,1)S(1)}, u32[]{:S(2)}, u32[]{:S(2)}) %collective-permute-start.3) | collective-permute-done | bytes 262176 | tf_op jit(solution)/shard_map/ppermute | solution.py:405
  67.2 5.1 %collective-permute-done.4.rest_3_ = bf16[2,128,512]{2,1,0:T(8,128)(2,1)S(1)} collective-permute-done((bf16[2,128,512]{2,1,0:T(8,128)(2,1)}, bf16[2,128,512]{2,1,0:T(8,128)(2,1)S(1)}, u32[]{:S(2)}, u32[]{:S(2)}) %collective-permute-start.4) | collective-permute-done | bytes 262176 | tf_op jit(solution)/shard_map/ppermute | solution.py:405
  72.3 0.7 copy-done.7
  73.0 5.2 %send_rows.1 = bf16[24,160,256]{2,1,0:T(8,128)(2,1)} custom-call(s32[1]{0:T(128)} %bitcast.where_ref, s32[24]{0:T(128)} %get-tuple-element.21.index_ref, s32[24]{0:T(128)} %get-tuple-element.20.valid_ref, bf16[2,128,512]{2,1,0:T(8,128)(2,1)} %get-tuple-element.10.rest_0_, bf16[2,128,512]{2,1,0:T(8,128)(2,1)} %copy-done.5, bf16[2,128,512]{2,1,0:T(8,128)(2,1)} %copy-done.6, ...), custom_call_target="tpu_custom_call" | custom-call | flops 4194304 | bytes 4194304 | tf_op jit(solution)/shard_map/send_rows/pallas_call | solution.py:333
  78.2 5.8 %all-to-all-start = ((bf16[24,160,256]{2,1,0:T(8,128)(2,1)}), bf16[24,160,256]{2,1,0:T(8,128)(2,1)S(1)}, u32[]{:S(2)}, u32[]{:S(2)}) async-start(bf16[24,160,256]{2,1,0:T(8,128)(2,1)} %send_rows.1), calls=%async_computation | async-start | bytes 3932160 | tf_op jit(solution)/shard_map/all_to_all | solution.py:433
  85.1 44.8 %all-to-all-done.source_ref = bf16[24,160,256]{2,1,0:T(8,128)(2,1)S(1)} async-done(((bf16[24,160,256]{2,1,0:T(8,128)(2,1)}), bf16[24,160,256]{2,1,0:T(8,128)(2,1)S(1)}, u32[]{:S(2)}, u32[]{:S(2)}) %all-to-all-start) | async-done | bytes 1966112 | tf_op jit(solution)/shard_map/all_to_all | solution.py:433
  130.0 1.3 copy-done
  131.3 3.5 %slot_rows.1 = bf16[24,160,256]{2,1,0:T(8,128)(2,1)} custom-call(s32[24]{0:T(128)} %get-tuple-element.19.index_ref, s32[24]{0:T(128)} %get-tuple-element.18.valid_ref, bf16[24,160,256]{2,1,0:T(8,128)(2,1)} %copy-done), custom_call_target="tpu_custom_call" | custom-call | flops 1048576 | bytes 4194304 | tf_op jit(solution)/shard_map/slot_rows/pallas_call | solution.py:364
  134.7 3.6 %all-to-all-start.1 = ((bf16[24,160,256]{2,1,0:T(8,128)(2,1)}), bf16[24,160,256]{2,1,0:T(8,128)(2,1)S(1)}, u32[]{:S(2)}, u32[]{:S(2)}) async-start(bf16[24,160,256]{2,1,0:T(8,128)(2,1)} %slot_rows.1), calls=%async_computation.1 | async-start | bytes 3932160 | tf_op jit(solution)/shard_map/all_to_all | solution.py:436
  138.4 5.1 %slab_rows.1 = f32[16,128,512]{2,1,0:T(8,128)} custom-call(s32[1]{0:T(128)} %bitcast.where_ref, bf16[2,128,512]{2,1,0:T(8,128)(2,1)} %get-tuple-element.10.rest_0_, bf16[2,128,512]{2,1,0:T(8,128)(2,1)} %copy-done.5, bf16[2,128,512]{2,1,0:T(8,128)(2,1)} %copy-done.6, bf16[2,128,512]{2,1,0:T(8,128)(2,1)} %copy-done.7, ...), custom_call_target="tpu_custom_call" | custom-call | flops 4194304 | bytes 6291456 | tf_op jit(solution)/shard_map/slab_rows/pallas_call | solution.py:291
  143.5 19.1 %all-to-all-done.1 = bf16[24,160,256]{2,1,0:T(8,128)(2,1)S(1)} async-done(((bf16[24,160,256]{2,1,0:T(8,128)(2,1)}), bf16[24,160,256]{2,1,0:T(8,128)(2,1)S(1)}, u32[]{:S(2)}, u32[]{:S(2)}) %all-to-all-start.1) | async-done | bytes 1966112 | tf_op jit(solution)/shard_map/all_to_all | solution.py:436
  162.6 1.3 copy-done.1
  163.9 5.8 %stack_rows.1 = f32[6,512,512]{2,1,0:T(8,128)} custom-call(bf16[4,6,160,256]{3,2,1,0:T(8,128)(2,1)} %bitcast.9), custom_call_target="tpu_custom_call" | custom-call | flops 4194304 | bytes 8388608 | tf_op jit(solution)/shard_map/stack_rows/pallas_call | solution.py:393
  (42 shorter events, 3.2 us)
Async XLA Ops:
  6.3 6.1 %collective-permute-start = (bf16[4,2,320,512]{3,2,1,0:T(8,128)(2,1)}, bf16[4,2,320,512]{3,2,1,0:T(8,128)(2,1)S(1)}, u32[]{:S(2)}, u32[]{:S(2)}) collective-permute-start(bf16[4,2,320,512]{3,2,1,0:T(8,128)(2,1)} %grams_1.1), channel_id=1, source_target_pairs={{0,8},{8,0},{16,24},{24,16},{1,9},{9,1},{17,25},{25,17},{2,10},{10... | collective-permute-start | bytes 7864328 | tf_op jit(solution)/shard_map/ppermute | solution.py:405
  12.4 6.0 %copy-start.9 = (s32[128]{0:T(128)S(1)}, s32[128]{0:T(128)}, u32[]{:S(2)}) copy-start(s32[128]{0:T(128)} %param.3) | copy-start | bytes 1540
  12.4 3.5 %copy-start.8 = (bf16[4,2,320,512]{3,2,1,0:T(8,128)(2,1)}, bf16[4,2,320,512]{3,2,1,0:T(8,128)(2,1)S(1)}, u32[]{:S(2)}) copy-start(bf16[4,2,320,512]{3,2,1,0:T(8,128)(2,1)S(1)} %collective-permute-done) | copy-start | bytes 7864324
  15.9 18.4 %collective-permute-start.5 = (bf16[2,320,512]{2,1,0:T(8,128)(2,1)}, bf16[2,320,512]{2,1,0:T(8,128)(2,1)}, u32[]{:S(2)}, u32[]{:S(2)}) collective-permute-start(bf16[2,320,512]{2,1,0:T(8,128)(2,1)} %get-tuple-element.22), channel_id=1, source_target_pairs={{0,16},{8,24},{16,0},{24,8},{1,17},{9,25},{17,1},{25,9},{2,18},{10... | collective-permute-start | bytes 1966088 | tf_op jit(solution)/shard_map/ppermute | solution.py:405
  18.3 29.8 %collective-permute-start.1 = (bf16[2,320,512]{2,1,0:T(8,128)(2,1)S(1)}, bf16[2,320,512]{2,1,0:T(8,128)(2,1)S(1)}, u32[]{:S(2)}, u32[]{:S(2)}) collective-permute-start(bf16[2,320,512]{2,1,0:T(8,128)(2,1)S(1)} %get-tuple-element.23), channel_id=1, source_target_pairs={{0,16},{8,24},{16,0},{24,8},{1,17},{9,25},{17,1},{25,9},{2,18},{10... | collective-permute-start | bytes 1966088 | tf_op jit(solution)/shard_map/ppermute | solution.py:405
  42.9 16.9 %collective-permute-start.6 = (bf16[2,128,512]{2,1,0:T(8,128)(2,1)}, bf16[2,128,512]{2,1,0:T(8,128)(2,1)S(1)}, u32[]{:S(2)}, u32[]{:S(2)}) collective-permute-start(bf16[2,128,512]{2,1,0:T(8,128)(2,1)} %get-tuple-element.15), channel_id=1, source_target_pairs={{0,8},{8,0},{16,24},{24,16},{1,9},{9,1},{17,25},{25,17},{2,10},{10... | collective-permute-start | bytes 786440 | tf_op jit(solution)/shard_map/ppermute | solution.py:405
  42.9 17.7 %collective-permute-start.7 = (bf16[2,128,512]{2,1,0:T(8,128)(2,1)}, bf16[2,128,512]{2,1,0:T(8,128)(2,1)S(1)}, u32[]{:S(2)}, u32[]{:S(2)}) collective-permute-start(bf16[2,128,512]{2,1,0:T(8,128)(2,1)} %get-tuple-element.16), channel_id=1, source_target_pairs={{0,16},{8,24},{16,0},{24,8},{1,17},{9,25},{17,1},{25,9},{2,18},{10... | collective-permute-start | bytes 786440 | tf_op jit(solution)/shard_map/ppermute | solution.py:405
  45.0 15.6 %collective-permute-start.8 = (bf16[2,128,512]{2,1,0:T(8,128)(2,1)}, bf16[2,128,512]{2,1,0:T(8,128)(2,1)S(1)}, u32[]{:S(2)}, u32[]{:S(2)}) collective-permute-start(bf16[2,128,512]{2,1,0:T(8,128)(2,1)} %get-tuple-element.17), channel_id=1, source_target_pairs={{0,24},{8,16},{16,8},{24,0},{1,25},{9,17},{17,9},{25,1},{2,26},{10... | collective-permute-start | bytes 786440 | tf_op jit(solution)/shard_map/ppermute | solution.py:405
  48.2 0.8 copy-start.10
  57.7 2.9 %collective-permute-start.2 = (bf16[2,128,512]{2,1,0:T(8,128)(2,1)}, bf16[2,128,512]{2,1,0:T(8,128)(2,1)S(1)}, u32[]{:S(2)}, u32[]{:S(2)}) collective-permute-start(bf16[2,128,512]{2,1,0:T(8,128)(2,1)} %get-tuple-element.11), channel_id=1, source_target_pairs={{0,8},{8,0},{16,24},{24,16},{1,9},{9,1},{17,25},{25,17},{2,10},{10... | collective-permute-start | bytes 786440 | tf_op jit(solution)/shard_map/ppermute | solution.py:405
  57.8 9.4 %collective-permute-start.3 = (bf16[2,128,512]{2,1,0:T(8,128)(2,1)}, bf16[2,128,512]{2,1,0:T(8,128)(2,1)S(1)}, u32[]{:S(2)}, u32[]{:S(2)}) collective-permute-start(bf16[2,128,512]{2,1,0:T(8,128)(2,1)} %get-tuple-element.12), channel_id=1, source_target_pairs={{0,16},{8,24},{16,0},{24,8},{1,17},{9,25},{17,1},{25,9},{2,18},{10... | collective-permute-start | bytes 786440 | tf_op jit(solution)/shard_map/ppermute | solution.py:405
  59.8 12.5 %copy-start.2 = (bf16[2,128,512]{2,1,0:T(8,128)(2,1)}, bf16[2,128,512]{2,1,0:T(8,128)(2,1)S(1)}, u32[]{:S(2)}) copy-start(bf16[2,128,512]{2,1,0:T(8,128)(2,1)S(1)} %collective-permute-done.6.rest_5_) | copy-start | bytes 786436
  59.8 12.5 %collective-permute-start.4 = (bf16[2,128,512]{2,1,0:T(8,128)(2,1)}, bf16[2,128,512]{2,1,0:T(8,128)(2,1)S(1)}, u32[]{:S(2)}, u32[]{:S(2)}) collective-permute-start(bf16[2,128,512]{2,1,0:T(8,128)(2,1)} %get-tuple-element.13), channel_id=1, source_target_pairs={{0,24},{8,16},{16,8},{24,0},{1,25},{9,17},{17,9},{25,1},{2,26},{10... | collective-permute-start | bytes 786440 | tf_op jit(solution)/shard_map/ppermute | solution.py:405
  60.6 11.7 %copy-start.3 = (bf16[2,128,512]{2,1,0:T(8,128)(2,1)}, bf16[2,128,512]{2,1,0:T(8,128)(2,1)S(1)}, u32[]{:S(2)}) copy-start(bf16[2,128,512]{2,1,0:T(8,128)(2,1)S(1)} %collective-permute-done.7.rest_6_) | copy-start | bytes 786436
  60.6 11.7 %copy-start.4 = (bf16[2,128,512]{2,1,0:T(8,128)(2,1)}, bf16[2,128,512]{2,1,0:T(8,128)(2,1)S(1)}, u32[]{:S(2)}) copy-start(bf16[2,128,512]{2,1,0:T(8,128)(2,1)S(1)} %collective-permute-done.8.rest_7_) | copy-start | bytes 786436
  60.7 11.7 %copy-start.5 = (bf16[2,128,512]{2,1,0:T(8,128)(2,1)}, bf16[2,128,512]{2,1,0:T(8,128)(2,1)S(1)}, u32[]{:S(2)}) copy-start(bf16[2,128,512]{2,1,0:T(8,128)(2,1)S(1)} %collective-permute-done.2.rest_1_) | copy-start | bytes 786436
  67.2 5.1 %copy-start.6 = (bf16[2,128,512]{2,1,0:T(8,128)(2,1)}, bf16[2,128,512]{2,1,0:T(8,128)(2,1)S(1)}, u32[]{:S(2)}) copy-start(bf16[2,128,512]{2,1,0:T(8,128)(2,1)S(1)} %collective-permute-done.3.rest_2_) | copy-start | bytes 786436
  72.3 0.7 copy-start.7
  78.2 51.8 %all-to-all-start = ((bf16[24,160,256]{2,1,0:T(8,128)(2,1)}), bf16[24,160,256]{2,1,0:T(8,128)(2,1)S(1)}, u32[]{:S(2)}, u32[]{:S(2)}) async-start(bf16[24,160,256]{2,1,0:T(8,128)(2,1)} %send_rows.1), calls=%async_computation | async-start | bytes 3932160 | tf_op jit(solution)/shard_map/all_to_all | solution.py:433
  130.0 1.3 copy-start
  134.7 27.8 %all-to-all-start.1 = ((bf16[24,160,256]{2,1,0:T(8,128)(2,1)}), bf16[24,160,256]{2,1,0:T(8,128)(2,1)S(1)}, u32[]{:S(2)}, u32[]{:S(2)}) async-start(bf16[24,160,256]{2,1,0:T(8,128)(2,1)} %slot_rows.1), calls=%async_computation.1 | async-start | bytes 3932160 | tf_op jit(solution)/shard_map/all_to_all | solution.py:436
  162.6 1.3 copy-start.1

commit v2 on v1

--- a/solution.py
+++ b/solution.py
@@ -1,3 +1,5 @@
+import functools
+
 import jax
 import jax.numpy as jnp
 from jax import lax
@@ -7,6 +9,8 @@
 
 ITERS = 3
 CAP = 24
+PARTS = 5
+MESH = pl.DeviceIdType.MESH
 
 
 def batched(first, second):
@@ -310,20 +314,23 @@
         @pl.when(valid_ref[place] > 0)
         def _():
             stat = index_ref[place]
-            out_ref[place, 0:128, 0:128] = held[stat, :, pl.ds(own, 128)]
-            out_ref[place, 0:128, 128:256] = held[stat, :, pl.ds(after, 128)]
+            for part in range(PARTS - 1):
+                rows = slice(part * 32, part * 32 + 32)
+                out_ref[part, place, :, 0:128] = held[stat, rows, pl.ds(own, 128)]
+                out_ref[part, place, :, 128:256] = held[stat, rows, pl.ds(after, 128)]
             tile = held[stat, :, pl.ds(across, 128)].astype(jnp.float32)
             half = jnp.where(device < 2, tile[0:64, :], tile.T[64:128, :]).astype(jnp.bfloat16)
-            out_ref[place, 128:160, 0:128] = half[0:32, :]
-            out_ref[place, 128:160, 128:256] = half[32:64, :]
+            out_ref[PARTS - 1, place, :, 0:128] = half[0:32, :]
+            out_ref[PARTS - 1, place, :, 128:256] = half[32:64, :]
 
         @pl.when(valid_ref[place] == 0)
         def _():
-            out_ref[place] = jnp.zeros(out_ref.shape[1:], out_ref.dtype)
+            for part in range(PARTS):
+                out_ref[part, place] = jnp.zeros(out_ref.shape[2:], out_ref.dtype)
 
         return carry
 
-    lax.fori_loop(0, out_ref.shape[0], body, 0)
+    lax.fori_loop(0, out_ref.shape[1], body, 0)
 
 
 def send_rows(where, index, valid, pieces, stats):
@@ -334,7 +341,7 @@
         send_kernel,
         in_specs=[smem] * 3 + [pl.BlockSpec(memory_space=pltpu.VMEM)] * 8,
         out_specs=pl.BlockSpec(memory_space=pltpu.VMEM),
-        out_shape=jax.ShapeDtypeStruct((places, 160, 256), jnp.bfloat16),
+        out_shape=jax.ShapeDtypeStruct((PARTS, places, 32, 256), jnp.bfloat16),
         scratch_shapes=[
             pltpu.VMEM((stats, 128, size), jnp.bfloat16),
             pltpu.VMEM((128, 128), jnp.float32),
@@ -344,56 +351,117 @@
     )(where, index, valid, *pieces)
 
 
-def slot_kernel(index_ref, valid_ref, source_ref, out_ref):
-    def body(slot, carry):
-        @pl.when(valid_ref[slot] > 0)
-        def _():
-            out_ref[slot] = source_ref[index_ref[slot]]
-
-        @pl.when(valid_ref[slot] == 0)
-        def _():
-            out_ref[slot] = jnp.zeros(out_ref.shape[1:], out_ref.dtype)
-
-        return carry
-
-    lax.fori_loop(0, out_ref.shape[0], body, 0)
-
-
-def slot_rows(index, valid, source):
+def route_kernel(pair_count, model_count, index_ref, valid_ref, sent_ref, out_ref, *scratch):
+    held, slots = scratch[:PARTS], scratch[PARTS : 2 * PARTS]
+    model_send, model_recv, data_send, data_recv = scratch[2 * PARTS :]
+    me, device = lax.axis_index("mp"), lax.axis_index("dp")
+    share = slots[0].shape[0] // 4
+    barrier = pltpu.get_barrier_semaphore()
+    for hop in range(1, model_count):
+        pl.semaphore_signal(
+            barrier, inc=1, device_id={"mp": lax.rem(me + hop, model_count)}, device_id_type=MESH
+        )
+    for relative in range(1, 4):
+        pl.semaphore_signal(barrier, inc=1, device_id={"dp": device ^ relative}, device_id_type=MESH)
+    pl.semaphore_wait(barrier, model_count + 2)
+
+    own = pl.ds(me * pair_count, pair_count)
+    to_owners = []
+    for part in range(PARTS):
+        for hop in range(1, model_count):
+            owner = lax.rem(me + hop, model_count)
+            copy = pltpu.make_async_remote_copy(
+                src_ref=sent_ref.at[part, pl.ds(owner * pair_count, pair_count)],
+                dst_ref=held[part].at[own],
+                send_sem=model_send.at[part, hop - 1],
+                recv_sem=model_recv.at[part, hop - 1],
+                device_id={"mp": owner},
+                device_id_type=MESH,
+            )
+            copy.start()
+            to_owners.append(copy)
+    for part in range(PARTS):
+        held[part][own] = sent_ref[part, own]
+
+    to_slots = []
+    for part in range(PARTS):
+        for hop in range(1, model_count):
+            to_owners[part * (model_count - 1) + hop - 1].wait_recv()
+
+        def place(slot, carry, part=part):
+            value = held[part][index_ref[slot]]
+            slots[part][slot] = jnp.where(valid_ref[slot] > 0, value, jnp.zeros_like(value))
+            return carry
+
+        lax.fori_loop(0, slots[part].shape[0], place, 0)
+        for relative in (3, 2, 1):
+            target = device ^ relative
+            copy = pltpu.make_async_remote_copy(
+                src_ref=slots[part].at[pl.ds(target * share, share)],
+                dst_ref=out_ref.at[part, device],
+                send_sem=data_send.at[part, relative - 1],
+                recv_sem=data_recv.at[part, relative - 1],
+                device_id={"dp": target},
+                device_id_type=MESH,
+            )
+            copy.start()
+            to_slots.append(copy)
+        out_ref[part, device] = slots[part][pl.ds(device * share, share)]
+    for copy in to_owners:
+        copy.wait_send()
+    for copy in to_slots:
+        copy.wait()
+
+
+def route(index, valid, sent, pair_count):
+    model_count = lax.axis_size("mp")
+    places = sent.shape[1]
+    slots = index.shape[0]
     smem = pl.BlockSpec(memory_space=pltpu.SMEM)
+    vmem = pl.BlockSpec(memory_space=pltpu.VMEM)
     return pl.pallas_call(
-        slot_kernel,
-        in_specs=[smem, smem, pl.BlockSpec(memory_space=pltpu.VMEM)],
-        out_specs=pl.BlockSpec(memory_space=pltpu.VMEM),
-        out_shape=jax.ShapeDtypeStruct((index.shape[0],) + source.shape[1:], source.dtype),
+        functools.partial(route_kernel, pair_count, model_count),
+        in_specs=[smem, smem, vmem],
+        out_specs=vmem,
+        out_shape=jax.ShapeDtypeStruct((PARTS, 4, slots // 4, 32, 256), jnp.bfloat16),
+        scratch_shapes=[pltpu.VMEM((places, 32, 256), jnp.bfloat16)] * PARTS
+        + [pltpu.VMEM((slots, 32, 256), jnp.bfloat16)] * PARTS
+        + [pltpu.SemaphoreType.DMA((PARTS, model_count - 1))] * 2
+        + [pltpu.SemaphoreType.DMA((PARTS, 3))] * 2,
+        compiler_params=pltpu.CompilerParams(collective_id=0, has_side_effects=True),
         cost_estimate=pl.CostEstimate(flops=2**20, bytes_accessed=4 * 2**20, transcendentals=0),
-        name="slot_rows",
-    )(index, valid, source)
+        name="route",
+    )(index, valid, sent)
 
 
 def stack_kernel(piece_ref, out_ref):
     tile_at = lambda i: slice(i * 128, i * 128 + 128)
+
+    def rows(i, lanes):
+        parts = [piece_ref[part, i, 0, :, lanes].astype(jnp.float32) for part in range(PARTS - 1)]
+        return jnp.concatenate(parts, axis=0)
+
     for i in range(4):
-        out_ref[0, tile_at(i), tile_at(i)] = opened(piece_ref[i, 0, 0:128, 0:128].astype(jnp.float32))
+        out_ref[0, tile_at(i), tile_at(i)] = opened(rows(i, slice(0, 128)))
         j = (i + 1) % 4
-        tile = piece_ref[i, 0, 0:128, 128:256].astype(jnp.float32)
+        tile = rows(i, slice(128, 256))
         out_ref[0, tile_at(i), tile_at(j)] = tile
         out_ref[0, tile_at(j), tile_at(i)] = tile.T
     for i in range(2):
         parts = []
         for source in (i, i + 2):
-            parts += [piece_ref[source, 0, 128:160, 0:128], piece_ref[source, 0, 128:160, 128:256]]
+            parts += [piece_ref[PARTS - 1, source, 0, :, 0:128], piece_ref[PARTS - 1, source, 0, :, 128:256]]
         tile = jnp.concatenate([part.astype(jnp.float32) for part in parts], axis=0)
         out_ref[0, tile_at(i), tile_at(i + 2)] = tile
         out_ref[0, tile_at(i + 2), tile_at(i)] = tile.T
 
 
 def stack_rows(pieces, size):
-    slots = pieces.shape[1]
+    slots = pieces.shape[2]
     return pl.pallas_call(
         stack_kernel,
         grid=(slots,),
-        in_specs=[pl.BlockSpec((4, 1, 160, 256), lambda slot: (0, slot, 0, 0))],
+        in_specs=[pl.BlockSpec((PARTS, 4, 1, 32, 256), lambda slot: (0, 0, slot, 0, 0))],
         out_specs=pl.BlockSpec((1, size, size), lambda slot: (slot, 0, 0)),
         out_shape=jax.ShapeDtypeStruct((slots, size, size), jnp.float32),
         cost_estimate=pl.CostEstimate(flops=2**22, bytes_accessed=8 * 2**20, transcendentals=0),
@@ -430,11 +498,8 @@
         roots = newton(where, own, received, far, chunk)
         pieces += [roots[0]] + [exchange(roots[relative], relative) for relative in (1, 2, 3)]
     sent = send_rows(where, send_index, send_valid, pieces, per_slab)
-    incoming = lax.all_to_all(sent, "mp", split_axis=0, concat_axis=0, tiled=True)
     slab = slab_rows(where, pieces, per_slab)
-    slots = slot_rows(stack_index, stack_valid, incoming)
-    shared = lax.all_to_all(slots, "dp", split_axis=0, concat_axis=0, tiled=True)
-    stacks = stack_rows(shared.reshape(4, CAP // 4, 160, 256), size)
+    stacks = stack_rows(route(stack_index, stack_valid, sent, pair_count), size)
     return (stacks[None], slab)
 
 

time: 170 us -> 146 us (0.86)
  waiting for transfers between devices: 93.9 us -> 29.4 us
  Pallas kernels: 48.3 us -> 100 us
  starting transfers between devices: 16.7 us -> 7.36 us
  local copies, waits for them, and re-layouts: 4.52 us -> 1.07 us
    all_to_all x2 -> x0, waiting for transfers between devices: 64 us -> none  [the longest x1 44.8 us: on_quad(): lax.all_to_all(sent, 'mp', split_axis=0, concat_axis=0, tiled=True)]
    pallas_call x2, Pallas kernels: 9.33 us -> 61.5 us  [the longest x1 55.6 us: route(): pl.pallas_call(functools.partial(route_kernel, pair_count, model_count),...]
    all_to_all x2 -> x0, starting transfers between devices: 9.41 us -> none  [the longest x1 5.81 us: on_quad(): lax.all_to_all(sent, 'mp', split_axis=0, concat_axis=0, tiled=True)]
    unnamed x22 -> x16, local copies, waits for them, and re-layouts: 4.14 us -> 0.69 us
  transfers between devices with their start and end apart: 11 -> 9, of which waited for: 6 -> 4; matrix products, arithmetic and copies ran while one was open for 1% -> 2% of each run, Pallas kernels for 17% -> 16%
where the time goes in v2:
time: 146 us; the launch traced here: 145 us
  Pallas kernels  100 us (68%)
  waiting for transfers between devices  29.4 us (20%)
  starting transfers between devices  7.36 us (5%)
  other arithmetic  5.63 us (4%)
    pallas_call x1, Pallas kernels, route(): pl.pallas_call(functools.partial(route_kernel, pair_count, model_count),...  55.6 us
    ppermute x9, waiting for transfers between devices, exchange(): return lax.ppermute(array, 'dp', [(i, i ^ relative) for i in range(4)])  29.4 us
    pallas_call x2, Pallas kernels, newton(): pl.pallas_call(newton_kernel, grid_spec=pltpu.PrefetchScalarGridSpec(num_...  17.3 us
    pallas_call x2, Pallas kernels, grams(): pl.pallas_call(gram_kernel, grid_spec=pltpu.PrefetchScalarGridSpec(num_sc...  11.2 us
    ppermute x9, starting transfers between devices, exchange(): return lax.ppermute(array, 'dp', [(i, i ^ relative) for i in range(4)])  7.36 us
    pallas_call x1, Pallas kernels, stack_rows(): pl.pallas_call(stack_kernel, grid=(slots,), in_specs=[pl.BlockSpec((PARTS...  5.87 us
    pallas_call x1, Pallas kernels, send_rows(): pl.pallas_call(send_kernel, in_specs=[smem] * 3 + [pl.BlockSpec(memory_sp...  5.19 us
    pallas_call x1, Pallas kernels, slab_rows(): pl.pallas_call(slab_kernel, in_specs=[pl.BlockSpec(memory_space=pltpu.SME...  5.1 us
  transfers between devices with their start and end apart: 9, of which 4 were waited for; matrix products, arithmetic and copies ran while one was open for 2% of the time, Pallas kernels for 16%

profile of v2, /device:TPU:0, one launch (start us, length us, event | category | flops | bytes accessed | tf_op | source)
XLA Modules:
  0.0 144.6 jit_solution(604828868283103256)
XLA Ops:
  0.6 5.6 %grams_1.1 = bf16[4,2,320,512]{3,2,1,0:T(8,128)(2,1)} custom-call(s32[1]{0:T(128)} %bitcast.where_ref, bf16[1,4096,512]{2,1,0:T(8,128)(2,1)} %grad_ref.3), custom_call_target="tpu_custom_call" | custom-call | flops 2147483648 | bytes 5242880 | tf_op jit(solution)/shard_map/grams_1/pallas_call | solution.py:158
  6.3 0.5 collective-permute-start
  6.9 5.6 %grams_0.1 = bf16[4,2,320,512]{3,2,1,0:T(8,128)(2,1)} custom-call(s32[1]{0:T(128)} %bitcast.where_ref, bf16[1,4096,512]{2,1,0:T(8,128)(2,1)} %grad_ref.3), custom_call_target="tpu_custom_call" | custom-call | flops 2147483648 | bytes 5242880 | tf_op jit(solution)/shard_map/grams_0/pallas_call | solution.py:158
  12.5 0.4 fusion.9
  13.0 3.5 %fusion.2 = (bf16[2,320,512]{2,1,0:T(8,128)(2,1)}, bf16[2,320,512]{2,1,0:T(8,128)(2,1)S(1)}) fusion(bf16[4,2,320,512]{3,2,1,0:T(8,128)(2,1)S(1)} %collective-permute-done, bf16[4,2,320,512]{3,2,1,0:T(8,128)(2,1)} %grams_0.1), kind=kLoop, calls=%fused_computation.5 | loop fusion | flops 2621440 | bytes 3932160 | tf_op jit(solution)/shard_map/convert_element_type | solution.py:496
  16.4 2.5 %collective-permute-start.5 = (bf16[2,320,512]{2,1,0:T(8,128)(2,1)}, bf16[2,320,512]{2,1,0:T(8,128)(2,1)}, u32[]{:S(2)}, u32[]{:S(2)}) collective-permute-start(bf16[2,320,512]{2,1,0:T(8,128)(2,1)} %get-tuple-element.22), channel_id=1, source_target_pairs={{0,16},{8,24},{16,0},{24,8},{1,17},{9,25},{17,1},{25,9},{2,18},{10... | collective-permute-start | bytes 1966088 | tf_op jit(solution)/shard_map/ppermute | solution.py:473
  19.2 0.2 reduce_window_sum.22
  19.4 15.4 %collective-permute-done.5.far_ref = bf16[2,320,512]{2,1,0:T(8,128)(2,1)} collective-permute-done((bf16[2,320,512]{2,1,0:T(8,128)(2,1)}, bf16[2,320,512]{2,1,0:T(8,128)(2,1)}, u32[]{:S(2)}, u32[]{:S(2)}) %collective-permute-start.5) | collective-permute-done | bytes 655392 | tf_op jit(solution)/shard_map/ppermute | solution.py:473
  34.8 8.7 %newton_1.1 = (bf16[2,128,512]{2,1,0:T(8,128)(2,1)}, bf16[2,128,512]{2,1,0:T(8,128)(2,1)}, bf16[2,128,512]{2,1,0:T(8,128)(2,1)}, bf16[2,128,512]{2,1,0:T(8,128)(2,1)}) custom-call(s32[1]{0:T(128)} %bitcast.where_ref, bf16[8,320,512]{2,1,0:T(8,128)(2,1)} %bitcast.11, bf16[8,320,512]{2,1,0:T(8,128)(2,1)} %bitcast.9, ...), custom_call_target="tpu_custom_call" | custom-call | flops 4294967296 | bytes 4194304 | tf_op jit(solution)/shard_map/newton_1/pallas_call | solution.py:235
  43.5 2.1 %collective-permute-start.7 = (bf16[2,128,512]{2,1,0:T(8,128)(2,1)}, bf16[2,128,512]{2,1,0:T(8,128)(2,1)S(1)}, u32[]{:S(2)}, u32[]{:S(2)}) collective-permute-start(bf16[2,128,512]{2,1,0:T(8,128)(2,1)} %get-tuple-element.16), channel_id=1, source_target_pairs={{0,16},{8,24},{16,0},{24,8},{1,17},{9,25},{17,1},{25,9},{2,18},{10... | collective-permute-start | bytes 786440 | tf_op jit(solution)/shard_map/ppermute | solution.py:473
  45.6 3.2 %collective-permute-done.1.far_ref = bf16[2,320,512]{2,1,0:T(8,128)(2,1)} collective-permute-done((bf16[2,320,512]{2,1,0:T(8,128)(2,1)S(1)}, bf16[2,320,512]{2,1,0:T(8,128)(2,1)}, u32[]{:S(2)}, u32[]{:S(2)}) %collective-permute-start.1) | collective-permute-done | bytes 655392 | tf_op jit(solution)/shard_map/ppermute | solution.py:473
  48.9 8.6 %newton_0.1 = (bf16[2,128,512]{2,1,0:T(8,128)(2,1)}, bf16[2,128,512]{2,1,0:T(8,128)(2,1)}, bf16[2,128,512]{2,1,0:T(8,128)(2,1)}, bf16[2,128,512]{2,1,0:T(8,128)(2,1)}) custom-call(s32[1]{0:T(128)} %bitcast.where_ref, bf16[8,320,512]{2,1,0:T(8,128)(2,1)} %bitcast.12, bf16[8,320,512]{2,1,0:T(8,128)(2,1)} %bitcast.10, ...), custom_call_target="tpu_custom_call" | custom-call | flops 4294967296 | bytes 4194304 | tf_op jit(solution)/shard_map/newton_0/pallas_call | solution.py:235
  57.5 2.1 %collective-permute-start.3 = (bf16[2,128,512]{2,1,0:T(8,128)(2,1)}, bf16[2,128,512]{2,1,0:T(8,128)(2,1)S(1)}, u32[]{:S(2)}, u32[]{:S(2)}) collective-permute-start(bf16[2,128,512]{2,1,0:T(8,128)(2,1)} %get-tuple-element.12), channel_id=1, source_target_pairs={{0,16},{8,24},{16,0},{24,8},{1,17},{9,25},{17,1},{25,9},{2,18},{10... | collective-permute-start | bytes 786440 | tf_op jit(solution)/shard_map/ppermute | solution.py:473
  59.6 0.1 collective-permute-start.4
  59.7 0.2 select_reduce_fusion
  60.0 0.7 convert_reduce_fusion
  60.6 0.7 convert_reduce_fusion.1
  61.3 5.6 %collective-permute-done.3.rest_2_ = bf16[2,128,512]{2,1,0:T(8,128)(2,1)S(1)} collective-permute-done((bf16[2,128,512]{2,1,0:T(8,128)(2,1)}, bf16[2,128,512]{2,1,0:T(8,128)(2,1)S(1)}, u32[]{:S(2)}, u32[]{:S(2)}) %collective-permute-start.3) | collective-permute-done | bytes 262176 | tf_op jit(solution)/shard_map/ppermute | solution.py:473
  67.0 5.1 %collective-permute-done.4.rest_3_ = bf16[2,128,512]{2,1,0:T(8,128)(2,1)S(1)} collective-permute-done((bf16[2,128,512]{2,1,0:T(8,128)(2,1)}, bf16[2,128,512]{2,1,0:T(8,128)(2,1)S(1)}, u32[]{:S(2)}, u32[]{:S(2)}) %collective-permute-start.4) | collective-permute-done | bytes 262176 | tf_op jit(solution)/shard_map/ppermute | solution.py:473
  72.1 0.7 copy-done.5
  72.8 5.2 %send_rows.1.sent_ref = bf16[5,24,32,256]{3,2,1,0:T(8,128)(2,1)} custom-call(s32[1]{0:T(128)} %bitcast.where_ref, s32[24]{0:T(128)} %get-tuple-element.21.index_ref, s32[24]{0:T(128)} %get-tuple-element.20.valid_ref, bf16[2,128,512]{2,1,0:T(8,128)(2,1)} %get-tuple-element.10.rest_0_, bf16[2,128,512]{2,1,0:T(8,128)(2,1)} %copy-done.3, ...), custom_call_target="tpu_custom_call" | custom-call | flops 4194304 | bytes 4194304 | tf_op jit(solution)/shard_map/send_rows/pallas_call | solution.py:340
  78.0 55.6 %route.1.piece_ref = bf16[5,4,6,32,256]{4,3,2,1,0:T(8,128)(2,1)} custom-call(s32[24]{0:T(128)} %get-tuple-element.19.index_ref, s32[24]{0:T(128)} %get-tuple-element.18.valid_ref, bf16[5,24,32,256]{3,2,1,0:T(8,128)(2,1)} %send_rows.1.sent_ref), custom_call_target="tpu_custom_call" | custom-call | flops 1048576 | bytes 4194304 | tf_op jit(solution)/shard_map/route/pallas_call | solution.py:422
  133.6 5.9 %stack_rows.1 = f32[6,512,512]{2,1,0:T(8,128)} custom-call(bf16[5,4,6,32,256]{4,3,2,1,0:T(8,128)(2,1)} %route.1.piece_ref), custom_call_target="tpu_custom_call" | custom-call | flops 4194304 | bytes 8388608 | tf_op jit(solution)/shard_map/stack_rows/pallas_call | solution.py:461
  139.5 5.1 %slab_rows.1 = f32[16,128,512]{2,1,0:T(8,128)} custom-call(s32[1]{0:T(128)} %bitcast.where_ref, bf16[2,128,512]{2,1,0:T(8,128)(2,1)} %get-tuple-element.10.rest_0_, bf16[2,128,512]{2,1,0:T(8,128)(2,1)} %copy-done.3, bf16[2,128,512]{2,1,0:T(8,128)(2,1)} %copy-done.4, bf16[2,128,512]{2,1,0:T(8,128)(2,1)} %copy-done.5, ...), custom_call_target="tpu_custom_call" | custom-call | flops 4194304 | bytes 6291456 | tf_op jit(solution)/shard_map/slab_rows/pallas_call | solution.py:295
  (32 shorter events, 0.6 us)
Async XLA Ops:
  0.6 6.1 %copy-start.7 = (s32[128]{0:T(128)S(1)}, s32[128]{0:T(128)}, u32[]{:S(2)}) copy-start(s32[128]{0:T(128)} %param.3) | copy-start | bytes 1540
  6.3 6.7 %collective-permute-start = (bf16[4,2,320,512]{3,2,1,0:T(8,128)(2,1)}, bf16[4,2,320,512]{3,2,1,0:T(8,128)(2,1)S(1)}, u32[]{:S(2)}, u32[]{:S(2)}) collective-permute-start(bf16[4,2,320,512]{3,2,1,0:T(8,128)(2,1)} %grams_1.1), channel_id=1, source_target_pairs={{0,8},{8,0},{16,24},{24,16},{1,9},{9,1},{17,25},{25,17},{2,10},{10... | collective-permute-start | bytes 7864328 | tf_op jit(solution)/shard_map/ppermute | solution.py:473
  13.0 21.9 %copy-start.6 = (bf16[4,2,320,512]{3,2,1,0:T(8,128)(2,1)}, bf16[4,2,320,512]{3,2,1,0:T(8,128)(2,1)S(1)}, u32[]{:S(2)}) copy-start(bf16[4,2,320,512]{3,2,1,0:T(8,128)(2,1)S(1)} %collective-permute-done) | copy-start | bytes 7864324
  16.4 18.4 %collective-permute-start.5 = (bf16[2,320,512]{2,1,0:T(8,128)(2,1)}, bf16[2,320,512]{2,1,0:T(8,128)(2,1)}, u32[]{:S(2)}, u32[]{:S(2)}) collective-permute-start(bf16[2,320,512]{2,1,0:T(8,128)(2,1)} %get-tuple-element.22), channel_id=1, source_target_pairs={{0,16},{8,24},{16,0},{24,8},{1,17},{9,25},{17,1},{25,9},{2,18},{10... | collective-permute-start | bytes 1966088 | tf_op jit(solution)/shard_map/ppermute | solution.py:473
  19.0 29.9 %collective-permute-start.1 = (bf16[2,320,512]{2,1,0:T(8,128)(2,1)S(1)}, bf16[2,320,512]{2,1,0:T(8,128)(2,1)}, u32[]{:S(2)}, u32[]{:S(2)}) collective-permute-start(bf16[2,320,512]{2,1,0:T(8,128)(2,1)S(1)} %get-tuple-element.23), channel_id=1, source_target_pairs={{0,16},{8,24},{16,0},{24,8},{1,17},{9,25},{17,1},{25,9},{2,18},{10... | collective-permute-start | bytes 1966088 | tf_op jit(solution)/shard_map/ppermute | solution.py:473
  43.5 16.1 %collective-permute-start.6 = (bf16[2,128,512]{2,1,0:T(8,128)(2,1)}, bf16[2,128,512]{2,1,0:T(8,128)(2,1)S(1)}, u32[]{:S(2)}, u32[]{:S(2)}) collective-permute-start(bf16[2,128,512]{2,1,0:T(8,128)(2,1)} %get-tuple-element.15), channel_id=1, source_target_pairs={{0,8},{8,0},{16,24},{24,16},{1,9},{9,1},{17,25},{25,17},{2,10},{10... | collective-permute-start | bytes 786440 | tf_op jit(solution)/shard_map/ppermute | solution.py:473
  43.5 17.8 %collective-permute-start.7 = (bf16[2,128,512]{2,1,0:T(8,128)(2,1)}, bf16[2,128,512]{2,1,0:T(8,128)(2,1)S(1)}, u32[]{:S(2)}, u32[]{:S(2)}) collective-permute-start(bf16[2,128,512]{2,1,0:T(8,128)(2,1)} %get-tuple-element.16), channel_id=1, source_target_pairs={{0,16},{8,24},{16,0},{24,8},{1,17},{9,25},{17,1},{25,9},{2,18},{10... | collective-permute-start | bytes 786440 | tf_op jit(solution)/shard_map/ppermute | solution.py:473
  45.6 15.7 %collective-permute-start.8 = (bf16[2,128,512]{2,1,0:T(8,128)(2,1)}, bf16[2,128,512]{2,1,0:T(8,128)(2,1)S(1)}, u32[]{:S(2)}, u32[]{:S(2)}) collective-permute-start(bf16[2,128,512]{2,1,0:T(8,128)(2,1)} %get-tuple-element.17), channel_id=1, source_target_pairs={{0,24},{8,16},{16,8},{24,0},{1,25},{9,17},{17,9},{25,1},{2,26},{10... | collective-permute-start | bytes 786440 | tf_op jit(solution)/shard_map/ppermute | solution.py:473
  57.5 3.8 %collective-permute-start.2 = (bf16[2,128,512]{2,1,0:T(8,128)(2,1)}, bf16[2,128,512]{2,1,0:T(8,128)(2,1)S(1)}, u32[]{:S(2)}, u32[]{:S(2)}) collective-permute-start(bf16[2,128,512]{2,1,0:T(8,128)(2,1)} %get-tuple-element.11), channel_id=1, source_target_pairs={{0,8},{8,0},{16,24},{24,16},{1,9},{9,1},{17,25},{25,17},{2,10},{10... | collective-permute-start | bytes 786440 | tf_op jit(solution)/shard_map/ppermute | solution.py:473
  57.5 9.4 %collective-permute-start.3 = (bf16[2,128,512]{2,1,0:T(8,128)(2,1)}, bf16[2,128,512]{2,1,0:T(8,128)(2,1)S(1)}, u32[]{:S(2)}, u32[]{:S(2)}) collective-permute-start(bf16[2,128,512]{2,1,0:T(8,128)(2,1)} %get-tuple-element.12), channel_id=1, source_target_pairs={{0,16},{8,24},{16,0},{24,8},{1,17},{9,25},{17,1},{25,9},{2,18},{10... | collective-permute-start | bytes 786440 | tf_op jit(solution)/shard_map/ppermute | solution.py:473
  59.6 12.5 %copy-start = (bf16[2,128,512]{2,1,0:T(8,128)(2,1)}, bf16[2,128,512]{2,1,0:T(8,128)(2,1)S(1)}, u32[]{:S(2)}) copy-start(bf16[2,128,512]{2,1,0:T(8,128)(2,1)S(1)} %collective-permute-done.6.rest_5_) | copy-start | bytes 786436
  59.6 12.5 %collective-permute-start.4 = (bf16[2,128,512]{2,1,0:T(8,128)(2,1)}, bf16[2,128,512]{2,1,0:T(8,128)(2,1)S(1)}, u32[]{:S(2)}, u32[]{:S(2)}) collective-permute-start(bf16[2,128,512]{2,1,0:T(8,128)(2,1)} %get-tuple-element.13), channel_id=1, source_target_pairs={{0,24},{8,16},{16,8},{24,0},{1,25},{9,17},{17,9},{25,1},{2,26},{10... | collective-permute-start | bytes 786440 | tf_op jit(solution)/shard_map/ppermute | solution.py:473
  61.3 10.8 %copy-start.1 = (bf16[2,128,512]{2,1,0:T(8,128)(2,1)}, bf16[2,128,512]{2,1,0:T(8,128)(2,1)S(1)}, u32[]{:S(2)}) copy-start(bf16[2,128,512]{2,1,0:T(8,128)(2,1)S(1)} %collective-permute-done.7.rest_6_) | copy-start | bytes 786436
  61.3 10.8 %copy-start.2 = (bf16[2,128,512]{2,1,0:T(8,128)(2,1)}, bf16[2,128,512]{2,1,0:T(8,128)(2,1)S(1)}, u32[]{:S(2)}) copy-start(bf16[2,128,512]{2,1,0:T(8,128)(2,1)S(1)} %collective-permute-done.8.rest_7_) | copy-start | bytes 786436
  61.3 10.8 %copy-start.3 = (bf16[2,128,512]{2,1,0:T(8,128)(2,1)}, bf16[2,128,512]{2,1,0:T(8,128)(2,1)S(1)}, u32[]{:S(2)}) copy-start(bf16[2,128,512]{2,1,0:T(8,128)(2,1)S(1)} %collective-permute-done.2.rest_1_) | copy-start | bytes 786436
  66.9 5.1 %copy-start.4 = (bf16[2,128,512]{2,1,0:T(8,128)(2,1)}, bf16[2,128,512]{2,1,0:T(8,128)(2,1)S(1)}, u32[]{:S(2)}) copy-start(bf16[2,128,512]{2,1,0:T(8,128)(2,1)S(1)} %collective-permute-done.3.rest_2_) | copy-start | bytes 786436
  72.1 0.7 copy-start.5

commit v3 on v2

--- a/solution.py
+++ b/solution.py
@@ -274,28 +274,30 @@
 
 def slab_kernel(where_ref, *rest):
     refs, out_ref = rest[:8], rest[8]
-    device = where_ref[0]
-    columns = pl.multiple_of(device * 128, 128)
-    for chunk in range(2):
-        for relative in range(4):
-            base = (device ^ relative) * 4 + chunk * 2
-
-            def body(place, carry):
-                value = refs[chunk * 4 + relative][place].astype(jnp.float32)
-                out_ref[base + place] = value
-                tile = refs[chunk * 4 + relative][place, :, pl.ds(columns, 128)].astype(jnp.float32)
-                out_ref[base + place, :, pl.ds(columns, 128)] = opened(tile)
-                return carry
-
-            lax.fori_loop(0, 2, body, 0)
+    columns = pl.multiple_of(where_ref[0] * 128, 128)
+    for source in range(8):
+
+        @pl.when(pl.program_id(0) == source)
+        def _(source=source):
+            for place in range(2):
+                out_ref[place] = refs[source][place].astype(jnp.float32)
+                tile = refs[source][place, :, pl.ds(columns, 128)].astype(jnp.float32)
+                out_ref[place, :, pl.ds(columns, 128)] = opened(tile)
 
 
 def slab_rows(where, pieces, stats):
     size = pieces[0].shape[-1]
     return pl.pallas_call(
         slab_kernel,
-        in_specs=[pl.BlockSpec(memory_space=pltpu.SMEM)] + [pl.BlockSpec(memory_space=pltpu.VMEM)] * 8,
-        out_specs=pl.BlockSpec(memory_space=pltpu.VMEM),
+        grid_spec=pltpu.PrefetchScalarGridSpec(
+            num_scalar_prefetch=1,
+            grid=(8,),
+            in_specs=[pl.BlockSpec((2, 128, size), lambda step, where_ref: (0, 0, 0))] * 8,
+            out_specs=pl.BlockSpec(
+                (2, 128, size),
+                lambda step, where_ref: ((where_ref[0] ^ (step % 4)) * 2 + step // 4, 0, 0),
+            ),
+        ),
         out_shape=jax.ShapeDtypeStruct((stats, 128, size), jnp.float32),
         cost_estimate=pl.CostEstimate(flops=2**22, bytes_accessed=6 * 2**20, transcendentals=0),
         name="slab_rows",

time: 146 us -> 146 us (level)
  no operation moved by 1% of the time
where the time goes in v3:
time: 146 us; the launch traced here: 145 us
  Pallas kernels  101 us (69%)
  waiting for transfers between devices  29.4 us (20%)
  starting transfers between devices  7.36 us (5%)
  other arithmetic  5.63 us (4%)
    pallas_call x1, Pallas kernels, route(): pl.pallas_call(functools.partial(route_kernel, pair_count, model_count),...  55.6 us
    ppermute x9, waiting for transfers between devices, exchange(): return lax.ppermute(array, 'dp', [(i, i ^ relative) for i in range(4)])  29.4 us
    pallas_call x2, Pallas kernels, newton(): pl.pallas_call(newton_kernel, grid_spec=pltpu.PrefetchScalarGridSpec(num_...  17.3 us
    pallas_call x2, Pallas kernels, grams(): pl.pallas_call(gram_kernel, grid_spec=pltpu.PrefetchScalarGridSpec(num_sc...  11.2 us
    ppermute x9, starting transfers between devices, exchange(): return lax.ppermute(array, 'dp', [(i, i ^ relative) for i in range(4)])  7.36 us
    pallas_call x1, Pallas kernels, stack_rows(): pl.pallas_call(stack_kernel, grid=(slots,), in_specs=[pl.BlockSpec((PARTS...  5.87 us
    pallas_call x1, Pallas kernels, slab_rows(): pl.pallas_call(slab_kernel, grid_spec=pltpu.PrefetchScalarGridSpec(num_sc...  5.41 us
    pallas_call x1, Pallas kernels, send_rows(): pl.pallas_call(send_kernel, in_specs=[smem] * 3 + [pl.BlockSpec(memory_sp...  5.19 us
  transfers between devices with their start and end apart: 9, of which 4 were waited for; matrix products, arithmetic and copies ran while one was open for 2% of the time, Pallas kernels for 16%

profile of v3, /device:TPU:0, one launch (start us, length us, event | category | flops | bytes accessed | tf_op | source)
XLA Modules:
  0.0 144.9 jit_solution(10586781720466634334)
XLA Ops:
  0.6 5.6 %grams_1.1 = bf16[4,2,320,512]{3,2,1,0:T(8,128)(2,1)} custom-call(s32[1]{0:T(128)} %bitcast.where_ref, bf16[1,4096,512]{2,1,0:T(8,128)(2,1)} %grad_ref.3), custom_call_target="tpu_custom_call" | custom-call | flops 2147483648 | bytes 5242880 | tf_op jit(solution)/shard_map/grams_1/pallas_call | solution.py:158
  6.3 0.5 collective-permute-start
  6.9 5.6 %grams_0.1 = bf16[4,2,320,512]{3,2,1,0:T(8,128)(2,1)} custom-call(s32[1]{0:T(128)} %bitcast.where_ref, bf16[1,4096,512]{2,1,0:T(8,128)(2,1)} %grad_ref.3), custom_call_target="tpu_custom_call" | custom-call | flops 2147483648 | bytes 5242880 | tf_op jit(solution)/shard_map/grams_0/pallas_call | solution.py:158
  12.5 0.4 fusion.9
  13.0 3.5 %fusion.2 = (bf16[2,320,512]{2,1,0:T(8,128)(2,1)}, bf16[2,320,512]{2,1,0:T(8,128)(2,1)S(1)}) fusion(bf16[4,2,320,512]{3,2,1,0:T(8,128)(2,1)S(1)} %collective-permute-done, bf16[4,2,320,512]{3,2,1,0:T(8,128)(2,1)} %grams_0.1), kind=kLoop, calls=%fused_computation.5 | loop fusion | flops 2621440 | bytes 3932160 | tf_op jit(solution)/shard_map/convert_element_type | solution.py:498
  16.4 2.5 %collective-permute-start.5 = (bf16[2,320,512]{2,1,0:T(8,128)(2,1)}, bf16[2,320,512]{2,1,0:T(8,128)(2,1)}, u32[]{:S(2)}, u32[]{:S(2)}) collective-permute-start(bf16[2,320,512]{2,1,0:T(8,128)(2,1)} %get-tuple-element.22), channel_id=1, source_target_pairs={{0,16},{8,24},{16,0},{24,8},{1,17},{9,25},{17,1},{25,9},{2,18},{10... | collective-permute-start | bytes 1966088 | tf_op jit(solution)/shard_map/ppermute | solution.py:475
  19.2 0.2 reduce_window_sum.22
  19.4 15.4 %collective-permute-done.5.far_ref = bf16[2,320,512]{2,1,0:T(8,128)(2,1)} collective-permute-done((bf16[2,320,512]{2,1,0:T(8,128)(2,1)}, bf16[2,320,512]{2,1,0:T(8,128)(2,1)}, u32[]{:S(2)}, u32[]{:S(2)}) %collective-permute-start.5) | collective-permute-done | bytes 655392 | tf_op jit(solution)/shard_map/ppermute | solution.py:475
  34.8 8.7 %newton_1.1 = (bf16[2,128,512]{2,1,0:T(8,128)(2,1)}, bf16[2,128,512]{2,1,0:T(8,128)(2,1)}, bf16[2,128,512]{2,1,0:T(8,128)(2,1)}, bf16[2,128,512]{2,1,0:T(8,128)(2,1)}) custom-call(s32[1]{0:T(128)} %bitcast.where_ref, bf16[8,320,512]{2,1,0:T(8,128)(2,1)} %bitcast.11, bf16[8,320,512]{2,1,0:T(8,128)(2,1)} %bitcast.9, ...), custom_call_target="tpu_custom_call" | custom-call | flops 4294967296 | bytes 4194304 | tf_op jit(solution)/shard_map/newton_1/pallas_call | solution.py:235
  43.5 2.1 %collective-permute-start.7 = (bf16[2,128,512]{2,1,0:T(8,128)(2,1)}, bf16[2,128,512]{2,1,0:T(8,128)(2,1)S(1)}, u32[]{:S(2)}, u32[]{:S(2)}) collective-permute-start(bf16[2,128,512]{2,1,0:T(8,128)(2,1)} %get-tuple-element.16), channel_id=1, source_target_pairs={{0,16},{8,24},{16,0},{24,8},{1,17},{9,25},{17,1},{25,9},{2,18},{10... | collective-permute-start | bytes 786440 | tf_op jit(solution)/shard_map/ppermute | solution.py:475
  45.6 3.2 %collective-permute-done.1.far_ref = bf16[2,320,512]{2,1,0:T(8,128)(2,1)} collective-permute-done((bf16[2,320,512]{2,1,0:T(8,128)(2,1)S(1)}, bf16[2,320,512]{2,1,0:T(8,128)(2,1)}, u32[]{:S(2)}, u32[]{:S(2)}) %collective-permute-start.1) | collective-permute-done | bytes 655392 | tf_op jit(solution)/shard_map/ppermute | solution.py:475
  48.9 8.6 %newton_0.1 = (bf16[2,128,512]{2,1,0:T(8,128)(2,1)}, bf16[2,128,512]{2,1,0:T(8,128)(2,1)}, bf16[2,128,512]{2,1,0:T(8,128)(2,1)}, bf16[2,128,512]{2,1,0:T(8,128)(2,1)}) custom-call(s32[1]{0:T(128)} %bitcast.where_ref, bf16[8,320,512]{2,1,0:T(8,128)(2,1)} %bitcast.12, bf16[8,320,512]{2,1,0:T(8,128)(2,1)} %bitcast.10, ...), custom_call_target="tpu_custom_call" | custom-call | flops 4294967296 | bytes 4194304 | tf_op jit(solution)/shard_map/newton_0/pallas_call | solution.py:235
  57.5 2.1 %collective-permute-start.3 = (bf16[2,128,512]{2,1,0:T(8,128)(2,1)}, bf16[2,128,512]{2,1,0:T(8,128)(2,1)S(1)}, u32[]{:S(2)}, u32[]{:S(2)}) collective-permute-start(bf16[2,128,512]{2,1,0:T(8,128)(2,1)} %get-tuple-element.12), channel_id=1, source_target_pairs={{0,16},{8,24},{16,0},{24,8},{1,17},{9,25},{17,1},{25,9},{2,18},{10... | collective-permute-start | bytes 786440 | tf_op jit(solution)/shard_map/ppermute | solution.py:475
  59.6 0.1 collective-permute-start.4
  59.7 0.2 select_reduce_fusion
  60.0 0.7 convert_reduce_fusion
  60.6 0.7 convert_reduce_fusion.1
  61.3 5.6 %collective-permute-done.3.rest_2_ = bf16[2,128,512]{2,1,0:T(8,128)(2,1)S(1)} collective-permute-done((bf16[2,128,512]{2,1,0:T(8,128)(2,1)}, bf16[2,128,512]{2,1,0:T(8,128)(2,1)S(1)}, u32[]{:S(2)}, u32[]{:S(2)}) %collective-permute-start.3) | collective-permute-done | bytes 262176 | tf_op jit(solution)/shard_map/ppermute | solution.py:475
  67.0 5.1 %collective-permute-done.4.rest_3_ = bf16[2,128,512]{2,1,0:T(8,128)(2,1)S(1)} collective-permute-done((bf16[2,128,512]{2,1,0:T(8,128)(2,1)}, bf16[2,128,512]{2,1,0:T(8,128)(2,1)S(1)}, u32[]{:S(2)}, u32[]{:S(2)}) %collective-permute-start.4) | collective-permute-done | bytes 262176 | tf_op jit(solution)/shard_map/ppermute | solution.py:475
  72.1 0.7 copy-done.5
  72.8 5.2 %send_rows.1.sent_ref = bf16[5,24,32,256]{3,2,1,0:T(8,128)(2,1)} custom-call(s32[1]{0:T(128)} %bitcast.where_ref, s32[24]{0:T(128)} %get-tuple-element.21.index_ref, s32[24]{0:T(128)} %get-tuple-element.20.valid_ref, bf16[2,128,512]{2,1,0:T(8,128)(2,1)} %get-tuple-element.10.rest_0_, bf16[2,128,512]{2,1,0:T(8,128)(2,1)} %copy-done.3, ...), custom_call_target="tpu_custom_call" | custom-call | flops 4194304 | bytes 4194304 | tf_op jit(solution)/shard_map/send_rows/pallas_call | solution.py:342
  78.0 55.6 %route.1.piece_ref = bf16[5,4,6,32,256]{4,3,2,1,0:T(8,128)(2,1)} custom-call(s32[24]{0:T(128)} %get-tuple-element.19.index_ref, s32[24]{0:T(128)} %get-tuple-element.18.valid_ref, bf16[5,24,32,256]{3,2,1,0:T(8,128)(2,1)} %send_rows.1.sent_ref), custom_call_target="tpu_custom_call" | custom-call | flops 1048576 | bytes 4194304 | tf_op jit(solution)/shard_map/route/pallas_call | solution.py:424
  133.6 5.9 %stack_rows.1 = f32[6,512,512]{2,1,0:T(8,128)} custom-call(bf16[5,4,6,32,256]{4,3,2,1,0:T(8,128)(2,1)} %route.1.piece_ref), custom_call_target="tpu_custom_call" | custom-call | flops 4194304 | bytes 8388608 | tf_op jit(solution)/shard_map/stack_rows/pallas_call | solution.py:463
  139.5 5.4 %slab_rows.1 = f32[16,128,512]{2,1,0:T(8,128)} custom-call(s32[1]{0:T(128)} %bitcast.where_ref, bf16[2,128,512]{2,1,0:T(8,128)(2,1)} %get-tuple-element.10.rest_0_, bf16[2,128,512]{2,1,0:T(8,128)(2,1)} %copy-done.3, bf16[2,128,512]{2,1,0:T(8,128)(2,1)} %copy-done.4, bf16[2,128,512]{2,1,0:T(8,128)(2,1)} %copy-done.5, ...), custom_call_target="tpu_custom_call" | custom-call | flops 4194304 | bytes 6291456 | tf_op jit(solution)/shard_map/slab_rows/pallas_call | solution.py:290
  (32 shorter events, 0.6 us)
Async XLA Ops:
  0.6 6.1 %copy-start.7 = (s32[128]{0:T(128)S(1)}, s32[128]{0:T(128)}, u32[]{:S(2)}) copy-start(s32[128]{0:T(128)} %param.3) | copy-start | bytes 1540
  6.3 6.7 %collective-permute-start = (bf16[4,2,320,512]{3,2,1,0:T(8,128)(2,1)}, bf16[4,2,320,512]{3,2,1,0:T(8,128)(2,1)S(1)}, u32[]{:S(2)}, u32[]{:S(2)}) collective-permute-start(bf16[4,2,320,512]{3,2,1,0:T(8,128)(2,1)} %grams_1.1), channel_id=1, source_target_pairs={{0,8},{8,0},{16,24},{24,16},{1,9},{9,1},{17,25},{25,17},{2,10},{10... | collective-permute-start | bytes 7864328 | tf_op jit(solution)/shard_map/ppermute | solution.py:475
  13.0 21.9 %copy-start.6 = (bf16[4,2,320,512]{3,2,1,0:T(8,128)(2,1)}, bf16[4,2,320,512]{3,2,1,0:T(8,128)(2,1)S(1)}, u32[]{:S(2)}) copy-start(bf16[4,2,320,512]{3,2,1,0:T(8,128)(2,1)S(1)} %collective-permute-done) | copy-start | bytes 7864324
  16.4 18.4 %collective-permute-start.5 = (bf16[2,320,512]{2,1,0:T(8,128)(2,1)}, bf16[2,320,512]{2,1,0:T(8,128)(2,1)}, u32[]{:S(2)}, u32[]{:S(2)}) collective-permute-start(bf16[2,320,512]{2,1,0:T(8,128)(2,1)} %get-tuple-element.22), channel_id=1, source_target_pairs={{0,16},{8,24},{16,0},{24,8},{1,17},{9,25},{17,1},{25,9},{2,18},{10... | collective-permute-start | bytes 1966088 | tf_op jit(solution)/shard_map/ppermute | solution.py:475
  19.0 29.9 %collective-permute-start.1 = (bf16[2,320,512]{2,1,0:T(8,128)(2,1)S(1)}, bf16[2,320,512]{2,1,0:T(8,128)(2,1)}, u32[]{:S(2)}, u32[]{:S(2)}) collective-permute-start(bf16[2,320,512]{2,1,0:T(8,128)(2,1)S(1)} %get-tuple-element.23), channel_id=1, source_target_pairs={{0,16},{8,24},{16,0},{24,8},{1,17},{9,25},{17,1},{25,9},{2,18},{10... | collective-permute-start | bytes 1966088 | tf_op jit(solution)/shard_map/ppermute | solution.py:475
  43.5 16.1 %collective-permute-start.6 = (bf16[2,128,512]{2,1,0:T(8,128)(2,1)}, bf16[2,128,512]{2,1,0:T(8,128)(2,1)S(1)}, u32[]{:S(2)}, u32[]{:S(2)}) collective-permute-start(bf16[2,128,512]{2,1,0:T(8,128)(2,1)} %get-tuple-element.15), channel_id=1, source_target_pairs={{0,8},{8,0},{16,24},{24,16},{1,9},{9,1},{17,25},{25,17},{2,10},{10... | collective-permute-start | bytes 786440 | tf_op jit(solution)/shard_map/ppermute | solution.py:475
  43.5 17.8 %collective-permute-start.7 = (bf16[2,128,512]{2,1,0:T(8,128)(2,1)}, bf16[2,128,512]{2,1,0:T(8,128)(2,1)S(1)}, u32[]{:S(2)}, u32[]{:S(2)}) collective-permute-start(bf16[2,128,512]{2,1,0:T(8,128)(2,1)} %get-tuple-element.16), channel_id=1, source_target_pairs={{0,16},{8,24},{16,0},{24,8},{1,17},{9,25},{17,1},{25,9},{2,18},{10... | collective-permute-start | bytes 786440 | tf_op jit(solution)/shard_map/ppermute | solution.py:475
  45.6 15.7 %collective-permute-start.8 = (bf16[2,128,512]{2,1,0:T(8,128)(2,1)}, bf16[2,128,512]{2,1,0:T(8,128)(2,1)S(1)}, u32[]{:S(2)}, u32[]{:S(2)}) collective-permute-start(bf16[2,128,512]{2,1,0:T(8,128)(2,1)} %get-tuple-element.17), channel_id=1, source_target_pairs={{0,24},{8,16},{16,8},{24,0},{1,25},{9,17},{17,9},{25,1},{2,26},{10... | collective-permute-start | bytes 786440 | tf_op jit(solution)/shard_map/ppermute | solution.py:475
  57.5 3.8 %collective-permute-start.2 = (bf16[2,128,512]{2,1,0:T(8,128)(2,1)}, bf16[2,128,512]{2,1,0:T(8,128)(2,1)S(1)}, u32[]{:S(2)}, u32[]{:S(2)}) collective-permute-start(bf16[2,128,512]{2,1,0:T(8,128)(2,1)} %get-tuple-element.11), channel_id=1, source_target_pairs={{0,8},{8,0},{16,24},{24,16},{1,9},{9,1},{17,25},{25,17},{2,10},{10... | collective-permute-start | bytes 786440 | tf_op jit(solution)/shard_map/ppermute | solution.py:475
  57.5 9.4 %collective-permute-start.3 = (bf16[2,128,512]{2,1,0:T(8,128)(2,1)}, bf16[2,128,512]{2,1,0:T(8,128)(2,1)S(1)}, u32[]{:S(2)}, u32[]{:S(2)}) collective-permute-start(bf16[2,128,512]{2,1,0:T(8,128)(2,1)} %get-tuple-element.12), channel_id=1, source_target_pairs={{0,16},{8,24},{16,0},{24,8},{1,17},{9,25},{17,1},{25,9},{2,18},{10... | collective-permute-start | bytes 786440 | tf_op jit(solution)/shard_map/ppermute | solution.py:475
  59.6 12.5 %copy-start = (bf16[2,128,512]{2,1,0:T(8,128)(2,1)}, bf16[2,128,512]{2,1,0:T(8,128)(2,1)S(1)}, u32[]{:S(2)}) copy-start(bf16[2,128,512]{2,1,0:T(8,128)(2,1)S(1)} %collective-permute-done.6.rest_5_) | copy-start | bytes 786436
  59.6 12.5 %collective-permute-start.4 = (bf16[2,128,512]{2,1,0:T(8,128)(2,1)}, bf16[2,128,512]{2,1,0:T(8,128)(2,1)S(1)}, u32[]{:S(2)}, u32[]{:S(2)}) collective-permute-start(bf16[2,128,512]{2,1,0:T(8,128)(2,1)} %get-tuple-element.13), channel_id=1, source_target_pairs={{0,24},{8,16},{16,8},{24,0},{1,25},{9,17},{17,9},{25,1},{2,26},{10... | collective-permute-start | bytes 786440 | tf_op jit(solution)/shard_map/ppermute | solution.py:475
  61.3 10.8 %copy-start.1 = (bf16[2,128,512]{2,1,0:T(8,128)(2,1)}, bf16[2,128,512]{2,1,0:T(8,128)(2,1)S(1)}, u32[]{:S(2)}) copy-start(bf16[2,128,512]{2,1,0:T(8,128)(2,1)S(1)} %collective-permute-done.7.rest_6_) | copy-start | bytes 786436
  61.3 10.8 %copy-start.2 = (bf16[2,128,512]{2,1,0:T(8,128)(2,1)}, bf16[2,128,512]{2,1,0:T(8,128)(2,1)S(1)}, u32[]{:S(2)}) copy-start(bf16[2,128,512]{2,1,0:T(8,128)(2,1)S(1)} %collective-permute-done.8.rest_7_) | copy-start | bytes 786436
  61.3 10.8 %copy-start.3 = (bf16[2,128,512]{2,1,0:T(8,128)(2,1)}, bf16[2,128,512]{2,1,0:T(8,128)(2,1)S(1)}, u32[]{:S(2)}) copy-start(bf16[2,128,512]{2,1,0:T(8,128)(2,1)S(1)} %collective-permute-done.2.rest_1_) | copy-start | bytes 786436
  66.9 5.1 %copy-start.4 = (bf16[2,128,512]{2,1,0:T(8,128)(2,1)}, bf16[2,128,512]{2,1,0:T(8,128)(2,1)S(1)}, u32[]{:S(2)}) copy-start(bf16[2,128,512]{2,1,0:T(8,128)(2,1)S(1)} %collective-permute-done.3.rest_2_) | copy-start | bytes 786436
  72.1 0.7 copy-start.5
